TPU v7x, 16 devices: a whole 2x2x2 slice. The times are simulated.
16 devices in a mesh: sp: 16 (over z, y, x, core).
Axes of the slice: x: 2, y: 2, z: 2, core: 2. Of those that a mesh axis runs over, the one named last changes fastest.
Arguments:
- x_in: bfloat16 [2, 2048, 3072], P(None, 'sp')
- grad_y: bfloat16 [2, 2048, 3072], P(None, 'sp')
- ln_gain: float32 [3072], replicated
- ln_bias: float32 [3072], replicated
- w_qkv: bfloat16 [3072, 3, 32, 96], replicated
- b_qkv: float32 [3, 32, 96], replicated
- w_out: bfloat16 [32, 96, 3072], replicated
- b_out: float32 [3072], replicated
Outputs:
- output 1: bfloat16 [2, 2048, 3072], P(None, 'sp')
- output 2: bfloat16 [2, 2048, 3072], P(None, 'sp')
- output 3: float32 [3072], replicated
- output 4: float32 [3072], replicated
- output 5: float32 [3072, 3, 32, 96], replicated
- output 6: float32 [3, 32, 96], replicated
- output 7: float32 [32, 96, 3072], replicated
- output 8: float32 [3072], replicated
All inputs are finite; a program needn't handle non-finite values.
Results may differ from a plain program's by a relative error of at most 0.0138752.
Values are sent between devices in bfloat16 or wider.
A program may use at most 1 GiB of HBM per device.

v0:
```python
import jax
import jax.numpy as jnp
from jax import lax
from jax.sharding import PartitionSpec as P

LN_EPS = 1e-5


def layer_norm_fwd(x_in, ln_gain, ln_bias):
    x_float = x_in.astype(jnp.float32)
    centered = x_float - jnp.mean(x_float, axis=-1, keepdims=True)
    inv_std = lax.rsqrt(jnp.mean(centered * centered, axis=-1, keepdims=True) + LN_EPS)
    x_hat = centered * inv_std
    normed = (x_hat * ln_gain + ln_bias).astype(jnp.bfloat16)
    return normed, x_hat, inv_std


def layer_norm_bwd(grad_normed, x_hat, inv_std, ln_gain):
    grad_hat = grad_normed * ln_gain
    mean_grad = jnp.mean(grad_hat, axis=-1, keepdims=True)
    mean_proj = jnp.mean(grad_hat * x_hat, axis=-1, keepdims=True)
    return inv_std * (grad_hat - mean_grad - x_hat * mean_proj)


def head_probs(qkv_head):
    attn_scale = qkv_head.shape[-1] ** -0.5
    positions = jnp.arange(qkv_head.shape[2])
    scores = jnp.einsum("crf,clf->crl", qkv_head[0], qkv_head[1], preferred_element_type=jnp.float32) * attn_scale
    scores = jnp.where(positions[:, None] >= positions[None, :], scores, -1e30)
    return jax.nn.softmax(scores, axis=-1)


def head_attention(qkv_head):
    prob_low = head_probs(qkv_head).astype(jnp.bfloat16)
    return jnp.einsum("crl,clf->crf", prob_low, qkv_head[2], preferred_element_type=jnp.float32).astype(jnp.bfloat16)


def head_attention_bwd(operands):
    qkv_head, grad_o = operands
    attn_scale = qkv_head.shape[-1] ** -0.5
    prob_f32 = head_probs(qkv_head)
    grad_v = jnp.einsum("crl,crf->clf", prob_f32.astype(jnp.bfloat16), grad_o, preferred_element_type=jnp.float32)
    grad_p = jnp.einsum("crf,clf->crl", grad_o, qkv_head[2], preferred_element_type=jnp.float32).astype(jnp.bfloat16).astype(jnp.float32)
    grad_s = (prob_f32 * (grad_p - jnp.sum(prob_f32 * grad_p, axis=-1, keepdims=True)) * attn_scale).astype(jnp.bfloat16)
    grad_q = jnp.einsum("crl,clf->crf", grad_s, qkv_head[1], preferred_element_type=jnp.float32)
    grad_k = jnp.einsum("crl,crf->clf", grad_s, qkv_head[0], preferred_element_type=jnp.float32)
    return jnp.stack([grad_q, grad_k, grad_v]).astype(jnp.bfloat16)


def solution(mesh):
    seq_spec = P(None, "sp", None)
    replicated = P()

    def local_block(x_in, grad_y, ln_gain, ln_bias, w_qkv, b_qkv, w_out, b_out):
        normed, x_hat, inv_std = layer_norm_fwd(x_in, ln_gain, ln_bias)
        bias_heads = jnp.transpose(b_qkv, (1, 0, 2))[:, :, None, None, :]
        qkv_local = (jnp.einsum("bsd,dthe->htbse", normed, w_qkv, preferred_element_type=jnp.float32) + bias_heads).astype(jnp.bfloat16)
        qkv_heads = lax.all_to_all(qkv_local, "sp", 0, 3, tiled=True)
        attn_heads = lax.map(head_attention, qkv_heads)
        attn_local = lax.all_to_all(attn_heads, "sp", 2, 0, tiled=True)
        proj_out = jnp.einsum("hbse,hed->bsd", attn_local, w_out, preferred_element_type=jnp.float32) + b_out
        y_out = (x_in.astype(jnp.float32) + proj_out).astype(jnp.bfloat16)
        grad_b_out = jnp.sum(grad_y, axis=(0, 1), dtype=jnp.float32)
        grad_w_out = jnp.einsum("hbse,bsd->hed", attn_local, grad_y, preferred_element_type=jnp.float32)
        grad_attn_local = jnp.einsum("bsd,hed->hbse", grad_y, w_out, preferred_element_type=jnp.float32).astype(jnp.bfloat16)
        grad_attn_heads = lax.all_to_all(grad_attn_local, "sp", 0, 2, tiled=True)
        grad_qkv_heads = lax.map(head_attention_bwd, (qkv_heads, grad_attn_heads))
        grad_qkv_local = lax.all_to_all(grad_qkv_heads, "sp", 3, 0, tiled=True)
        grad_b_qkv = jnp.transpose(jnp.sum(grad_qkv_local, axis=(2, 3), dtype=jnp.float32), (1, 0, 2))
        grad_w_qkv = jnp.einsum("bsd,htbse->dthe", normed, grad_qkv_local, preferred_element_type=jnp.float32)
        grad_normed = jnp.einsum("htbse,dthe->bsd", grad_qkv_local, w_qkv, preferred_element_type=jnp.float32).astype(jnp.bfloat16).astype(jnp.float32)
        grad_ln_gain = jnp.sum(grad_normed * x_hat, axis=(0, 1))
        grad_ln_bias = jnp.sum(grad_normed, axis=(0, 1))
        grad_x = (grad_y.astype(jnp.float32) + layer_norm_bwd(grad_normed, x_hat, inv_std, ln_gain)).astype(jnp.bfloat16)
        param_grads = lax.psum((grad_ln_gain, grad_ln_bias, grad_w_qkv, grad_b_qkv, grad_w_out, grad_b_out), "sp")
        return (y_out, grad_x) + tuple(param_grads)

    return jax.shard_map(local_block, mesh=mesh, in_specs=(seq_spec, seq_spec, replicated, replicated, replicated, replicated, replicated, replicated), out_specs=(seq_spec, seq_spec, replicated, replicated, replicated, replicated, replicated, replicated), check_vma=False)
```

profile of v0, /device:TPU:0, one launch (start us, length us, event | category | flops | bytes accessed | tf_op | source)
XLA Modules:
  0.0 2039.3 jit_solution(2541591402868475123)
XLA Ops:
  7.2 10.5 fusion.111
  17.7 5.3 all-to-all-start.2
  23.9 23.2 %fusion.70 = bf16[32,3,2,128,96]{3,4,0,1,2:T(8,128)(2,1)S(1)} fusion(f32[32,3,96]{2,0,1:T(8,128)S(1)} %bitcast.215, bf16[2,128,3072]{2,1,0:T(8,128)(2,1)S(1)} %copy-done, f32[3072]{0:T(1024)S(1)} %copy-done.11, f32[3072]{0:T(1024)S(1)} %copy-done.5, f32[2,128]{1,0:T(2,128)S(1)} %add_rsqrt_fusion, f32[2,128]{1,0:T(2,128)S(1)} %broadcast_multiply_fusion.2, ...), kind=kOutput, calls=%fused_computation.81 | convolution fusion | flops 14504951808 | bytes 62978048 | tf_op jit(solution)/shard_map/bsd,dthe->htbse/dot_general | solution.py:57
  47.1 3.5 copy.32
  50.6 3.9 all-to-all-start
  54.6 1.6 copy.79
  56.1 59.0 %all-to-all-done = bf16[32,3,2,128,96]{3,4,1,2,0:T(8,128)(2,1)} async-done(((bf16[32,3,2,128,96]{3,4,1,2,0:T(8,128)(2,1)}), bf16[32,3,2,128,96]{3,4,1,2,0:T(8,128)(2,1)}, u32[]{:S(2)}, u32[]{:S(2)}) %all-to-all-start) | async-done | bytes 4718624 | tf_op jit(solution)/shard_map/all_to_all | solution.py:58
  115.1 7.6 copy.33
  122.7 8.2 all_to_all.55
  130.9 236.0 %while.21 = (s32[]{:T(128)}, bf16[2,3,2,2048,96]{3,4,2,1,0:T(8,128)(2,1)}, bf16[2,3,2,2048,96]{3,4,2,1,0:T(8,128)(2,1)}, bf16[2,2,2048,96]{2,3,1,0:T(8,128)(2,1)}, s32[]{:T(128)}, /*index=5*/s32[]{:T(128)}, s32[]{}, s32[]{}) while((s32[]{:T(128)}, bf16[2,3,2,2048,96]{3,4,2,1,0:T(8,128)(2,1)}, bf16[2,3,2,2048,96]{3,4,2,1,0:T(8,128)(2,1)}, ...), condition=%wide.region_10.11_spmd, body=%wide.region_6.0_spmd.sunk | while | flops 8275245056 | bytes 306285696 | solution.py:67
  131.0 4.1 iota_compare_fusion.5
  135.1 19.6 fusion.140
  154.7 13.5 fusion.141
  168.2 12.1 convolution_convert_fusion.2
  180.4 33.5 %fusion.142 = bf16[1,1,2,2048,96]{3,4,2,1,0:T(8,128)(2,1)S(1)} fusion(bf16[2,2048,2048]{1,2,0:T(8,128)(2,1)} %convolution_convert_fusion.2, bf16[2,3,2,2048,96]{3,4,2,1,0:T(8,128)(2,1)} %get-tuple-element.187, s32[]{:T(128)S(6)} %copy.91, f32[2,2048,2048]{1,2,0:T(8,128)} %get-tuple-element.146, f32[2,2048]{1,0:T(2,128)S(1)} %get-tuple-element.147), kind=kOutput, calls=%fused_computation.49.clone.1 | convolution fusion | flops 1686509568 | bytes 102268928 | tf_op jit(solution)/shard_map/while/body/eval_jaxpr/crl,crf->clf/dot_general | solution.py:46
  213.9 33.4 %fusion.143 = bf16[1,1,2,2048,96]{3,4,2,1,0:T(8,128)(2,1)S(1)} fusion(bf16[2,2048,2048]{1,2,0:T(8,128)(2,1)} %convolution_convert_fusion.2, bf16[2,3,2,2048,96]{3,4,2,1,0:T(8,128)(2,1)} %get-tuple-element.187, s32[]{:T(128)S(6)} %copy.91, s32[]{:T(128)S(6)} %add.117, f32[2,2048,2048]{1,2,0:T(8,128)} %get-tuple-element.146, ...), kind=kOutput, calls=%fused_computation.50.clone.1 | convolution fusion | flops 1686509568 | bytes 102268936 | tf_op jit(solution)/shard_map/while/body/eval_jaxpr/crl,clf->crf/dot_general | solution.py:45
  248.8 4.1 iota_compare_fusion.5
  253.0 19.6 fusion.140
  272.5 13.5 fusion.141
  286.1 12.1 convolution_convert_fusion.2
  298.2 33.5 %fusion.142 = bf16[1,1,2,2048,96]{3,4,2,1,0:T(8,128)(2,1)S(1)} fusion(bf16[2,2048,2048]{1,2,0:T(8,128)(2,1)} %convolution_convert_fusion.2, bf16[2,3,2,2048,96]{3,4,2,1,0:T(8,128)(2,1)} %get-tuple-element.187, s32[]{:T(128)S(6)} %copy.91, f32[2,2048,2048]{1,2,0:T(8,128)} %get-tuple-element.146, f32[2,2048]{1,0:T(2,128)S(1)} %get-tuple-element.147), kind=kOutput, calls=%fused_computation.49.clone.1 | convolution fusion | flops 1686509568 | bytes 102268928 | tf_op jit(solution)/shard_map/while/body/eval_jaxpr/crl,crf->clf/dot_general | solution.py:46
  331.7 33.4 %fusion.143 = bf16[1,1,2,2048,96]{3,4,2,1,0:T(8,128)(2,1)S(1)} fusion(bf16[2,2048,2048]{1,2,0:T(8,128)(2,1)} %convolution_convert_fusion.2, bf16[2,3,2,2048,96]{3,4,2,1,0:T(8,128)(2,1)} %get-tuple-element.187, s32[]{:T(128)S(6)} %copy.91, s32[]{:T(128)S(6)} %add.117, f32[2,2048,2048]{1,2,0:T(8,128)} %get-tuple-element.146, ...), kind=kOutput, calls=%fused_computation.50.clone.1 | convolution fusion | flops 1686509568 | bytes 102268936 | tf_op jit(solution)/shard_map/while/body/eval_jaxpr/crl,clf->crf/dot_general | solution.py:45
  366.8 15.9 copy.37
  382.7 76.9 %all_to_all.72 = bf16[2,3,2,2048,96]{4,2,1,0,3:T(2,128)(2,1)} all-to-all(bf16[2,3,2,2048,96]{4,2,1,0,3:T(2,128)(2,1)} %copy.37), channel_id=1, replica_groups=mesh['sp'=16] {'sp'}, dimensions={3} | all-to-all | bytes 9437184 | tf_op jit(solution)/shard_map/all_to_all | solution.py:68
  459.7 15.8 copy.63
  475.5 40.9 %fusion.107 = f32[32,3,96,3072,1]{3,2,0,1,4:T(8,128)} fusion(bf16[32,3,2,128,96]{3,4,0,1,2:T(8,128)(2,1)} %bitcast.207, bf16[2,128,3072]{2,1,0:T(8,128)(2,1)S(1)} %copy-done.1, f32[3072]{0:T(1024)S(1)} %copy-done.12, f32[3072]{0:T(1024)S(1)} %copy-done.6, f32[2,128]{1,0:T(2,128)S(1)} %copy-done.16, f32[2,128]{1,0:T(2,128)S(1)} %copy-done.9), kind=kOutput, calls=%fused_computation.114 | convolution fusion | flops 14500233216 | bytes 119564288 | tf_op jit(solution)/shard_map/bsd,htbse->dthe/dot_general | solution.py:70
  516.4 74.6 %copy.78 = f32[32,3,96,3072,1]{3,2,1,0,4:T(8,128)} copy(f32[32,3,96,3072,1]{3,2,0,1,4:T(8,128)} %fusion.107) | data formatting | bytes 226492416 | tf_op jit(solution)/shard_map/bsd,htbse->dthe/dot_general | solution.py:70
  591.0 72.1 %while.20 = (s32[]{:T(128)}, bf16[2,2,2048,96]{2,3,1,0:T(8,128)(2,1)S(1)}, bf16[2,3,2,2048,96]{3,4,2,1,0:T(8,128)(2,1)}, s32[]{:T(128)}, s32[]{:T(128)}, /*index=5*/s32[]{}, s32[]{}) while((s32[]{:T(128)}, bf16[2,2,2048,96]{2,3,1,0:T(8,128)(2,1)S(1)}, bf16[2,3,2,2048,96]{3,4,2,1,0:T(8,128)(2,1)}, s32[]{:T(128)}, s32[]{:T(128)}, /*index=5*/s32[]{}, ...), condition=%wide.region_5.6_spmd, body=%wide.region_2.5_spmd.sunk | while | flops 3276146688 | bytes 78679152 | solution.py:59
  591.1 4.1 iota_compare_fusion.4
  595.2 19.6 fusion.135
  614.8 12.3 fusion.136
  627.1 4.1 iota_compare_fusion.4
  631.2 19.6 fusion.135
  650.8 12.3 fusion.136
  664.3 4.6 copy.34
  668.9 52.7 %all_to_all.73 = bf16[2,2,2048,96]{3,1,0,2:T(2,128)(2,1)} all-to-all(bf16[2,2,2048,96]{3,1,0,2:T(2,128)(2,1)S(1)} %copy.34), channel_id=1, replica_groups=mesh['sp'=16] {'sp'}, dimensions={2} | all-to-all | bytes 3145728 | tf_op jit(solution)/shard_map/all_to_all | solution.py:60
  721.6 4.7 copy.35
  726.4 15.5 copy.59
  741.9 15.6 copy.38
  757.5 4.2 convert_reduce_fusion
  762.3 25.4 %fusion.102 = (f32[3072]{0:T(1024)}, f32[2,128]{1,0:T(2,128)S(1)}, f32[2,128]{1,0:T(2,128)S(1)}, f32[3072]{0:T(1024)}, bf16[2,128,3072]{2,1,0:T(8,128)(2,1)}) fusion(bf16[2,128,3072]{2,1,0:T(8,128)(2,1)S(1)} %copy-done.2, f32[2,128]{1,0:T(2,128)S(1)} %copy-done.17, f32[2,128]{1,0:T(2,128)S(1)} %copy-done.10, f32[3072]{0:T(1024)S(1)} %copy-done.7, ...), kind=kOutput, calls=%fused_computation.110 | convolution fusion | flops 14504945664 | bytes 64528384 | tf_op jit(solution)/shard_map/htbse,dthe->bsd/dot_general | solution.py:71
  787.7 5.0 convert_reduce_fusion.3
  792.8 16.1 convolution_bitcast_fusion
  809.6 10.5 fusion.88
  820.1 753.8 %all-reduce.5.cloned.1.call-done = f32[3072,3,32,96]{0,3,1,2:T(8,128)} async-done(((f32[3072,3,32,96]{0,3,1,2:T(8,128)}), f32[3072,3,32,96]{0,3,1,2:T(8,128)}) %all-reduce.5.cloned.1.call-update) | async-done | bytes 113246224 | tf_op jit(solution)/shard_map/psum | solution.py:75
  1573.9 74.2 %copy.43 = f32[3072,3,32,96]{0,3,2,1:T(8,128)} copy(f32[3072,3,32,96]{0,3,1,2:T(8,128)} %all-reduce.5.cloned.1.call-done) | data formatting | bytes 226492416
  1648.1 351.8 %all-reduce.7.cloned.1.call-done = f32[32,96,3072]{2,1,0:T(8,128)} async-done(((f32[32,96,3072]{2,1,0:T(8,128)}), f32[32,96,3072]{2,1,0:T(8,128)}) %all-reduce.7.cloned.1.call-update) | async-done | bytes 37748752 | tf_op jit(solution)/shard_map/psum | solution.py:75
  2003.9 28.1 %copy.104 = f32[32,96,3072]{2,1,0:T(8,128)} copy(f32[32,96,3072]{2,1,0:T(8,128)} %all-reduce.7.cloned.1.call-done) | data formatting | bytes 75497472
  (60 shorter events, 11.3 us)
Async XLA Ops:
  7.2 15.8 copy-start
  17.7 6.2 copy-start.5
  17.7 6.2 copy-start.11
  17.7 6.2 copy-start.18
  17.7 32.9 %all-to-all-start.2 = ((bf16[32,2,128,96]{2,3,1,0:T(8,128)(2,1)}), bf16[32,2,128,96]{2,3,1,0:T(8,128)(2,1)S(1)}, u32[]{:S(2)}, u32[]{:S(2)}) async-start(bf16[32,2,128,96]{2,3,1,0:T(8,128)(2,1)} %fusion.111), calls=%async_computation.2 | async-start | bytes 3145728 | tf_op jit(solution)/shard_map/all_to_all | solution.py:66
  23.3 23.8 %copy-start.8 = (f32[2,128]{1,0:T(2,128)}, f32[2,128]{1,0:T(2,128)S(1)}, u32[]{:S(2)}) copy-start(f32[2,128]{1,0:T(2,128)S(1)} %broadcast_multiply_fusion.2) | copy-start | bytes 3076
  23.9 23.2 %copy-start.15 = (f32[2,128]{1,0:T(2,128)}, f32[2,128]{1,0:T(2,128)S(1)}, u32[]{:S(2)}) copy-start(f32[2,128]{1,0:T(2,128)S(1)} %add_rsqrt_fusion) | copy-start | bytes 3076
  50.6 64.5 %all-to-all-start = ((bf16[32,3,2,128,96]{3,4,1,2,0:T(8,128)(2,1)}), bf16[32,3,2,128,96]{3,4,1,2,0:T(8,128)(2,1)}, u32[]{:S(2)}, u32[]{:S(2)}) async-start(bf16[32,3,2,128,96]{3,4,1,2,0:T(8,128)(2,1)} %copy.32), calls=%async_computation | async-start | bytes 9437184 | tf_op jit(solution)/shard_map/all_to_all | solution.py:58
  54.5 1519.4 %all-reduce.5.cloned.1.call-start = ((), (), s32[]{:S(2)}) async-start(), calls=%async_computation.4 | async-start | bytes 226492416 | tf_op jit(solution)/shard_map/psum | solution.py:75
  459.7 15.8 copy-start.1
  459.7 15.8 copy-start.6
  459.7 15.8 copy-start.9
  459.7 15.8 copy-start.12
  459.7 15.8 copy-start.16
  591.0 1057.1 %all-reduce.9.cloned.1.call-start = ((), (), s32[]{:S(2)}) async-start(), calls=%async_computation.6 | async-start | bytes 172032 | tf_op jit(solution)/shard_map/psum | solution.py:75
  663.1 1.1 copy-start.4
  757.5 4.8 copy-start.2
  757.5 4.8 copy-start.7
  757.5 4.8 copy-start.10
  757.5 4.8 copy-start.17
  762.3 25.4 %copy-start.3 = (bf16[2,128,3072]{2,1,0:T(8,128)(2,1)S(1)}, bf16[2,128,3072]{2,1,0:T(8,128)(2,1)}, u32[]{:S(2)}) copy-start(bf16[2,128,3072]{2,1,0:T(8,128)(2,1)} %param.13) | copy-start | bytes 4718596
  792.7 1207.2 %all-reduce.7.cloned.1.call-start = ((), (), s32[]{:S(2)}) async-start(), calls=%async_computation.5 | async-start | bytes 75497472 | tf_op jit(solution)/shard_map/psum | solution.py:75
  808.9 0.7 copy-start.13
  2003.9 28.1 %copy-start.14 = (f32[3072]{0:T(1024)S(1)}, f32[3072]{0:T(1024)}, u32[]{:S(2)}) copy-start(f32[3072]{0:T(1024)} %get-tuple-element.200) | copy-start | bytes 36868
Sparse Core Ops, SparseCore 0:
  591.1 982.7 all-reduce.4
  1579.3 66.2 all-reduce.8
  1651.9 347.9 all-reduce.6
where the time goes:
time: 2050 us; the launch traced here: 2040 us
  waiting for transfers between devices  1160 us (57%)
  matrix products  414 us (20%)
  local copies, waits for them, and re-layouts  277 us (14%)
  blocking collectives  130 us (6%)
  other arithmetic  29.7 us (1%)
    psum x3, waiting for transfers between devices, local_block(): lax.psum((grad_ln_gain, grad_ln_bias, grad_w_qkv, grad_b_qkv, grad_w_out,...  1110 us
    unnamed x44, local copies, waits for them, and re-layouts  109 us
    sub x4, matrix products, head_probs(): return jax.nn.softmax(scores, axis=-1)  78.2 us
    all_to_all x1, blocking collectives, local_block(): grad_qkv_local = lax.all_to_all(grad_qkv_heads, 'sp', 3, 0, tiled=True)  76.9 us
    dot_general x1, local copies, waits for them, and re-layouts, local_block(): jnp.einsum('bsd,htbse->dthe', normed, grad_qkv_local, preferred_element_t...  74.6 us
    dot_general x2, matrix products, head_attention_bwd(): jnp.einsum('crl,crf->clf', grad_s, qkv_head[0], preferred_element_type=jn...  67 us
    dot_general x2, matrix products, head_attention_bwd(): jnp.einsum('crl,clf->crf', grad_s, qkv_head[1], preferred_element_type=jn...  66.7 us
    all_to_all x1, waiting for transfers between devices, local_block(): qkv_heads = lax.all_to_all(qkv_local, 'sp', 0, 3, tiled=True)  59 us
  transfers between devices with their start and end apart: 5, of which 3 were waited for; matrix products, arithmetic and copies ran while one was open for 14% of the time, Pallas kernels for 0%

commit v1 on v0

v1 whole, which is shorter than its diff:
```python
import functools
import math

import jax
import jax.numpy as jnp
from jax import lax
from jax.experimental import pallas as pl
from jax.experimental.pallas import tpu as pltpu
from jax.sharding import PartitionSpec as P


LN_EPS = 1e-5
F32 = jnp.float32
BF16 = jnp.bfloat16
VMEM_LIMIT = 64 * 1024 * 1024 - 65536

B, S, D, NH, DH = 2, 2048, 3072, 32, 96
NDEV = 16
TOK = S // NDEV
GH = 4
GR = GH * DH
CR = 4 * GR
SCALE = DH ** -0.5
BQ = 512


def dot_nt(a, b):
    return lax.dot_general(a, b, (((1,), (1,)), ((), ())), preferred_element_type=F32)


def dot_nn(a, b):
    return jnp.dot(a, b, preferred_element_type=F32)


def params(**kw):
    return pltpu.CompilerParams(vmem_limit_bytes=VMEM_LIMIT, **kw)


def proj_kernel(wt_ref, wo_ref, bias_ref, s_ref, qkv_ref, do_ref):
    u = jnp.concatenate([s_ref[0, :TOK], s_ref[1, :TOK]], axis=0)
    gy = jnp.concatenate([s_ref[0, TOK:], s_ref[1, TOK:]], axis=0)
    qkv_ref[...] = (dot_nt(wt_ref[...], u) + bias_ref[...]).astype(BF16)
    do_ref[...] = dot_nt(wo_ref[...], gy).astype(BF16)


def project(wt, wo, bias, gathered):
    full = lambda i: (0, 0)
    return pl.pallas_call(
        proj_kernel,
        grid=(NDEV // 2,),
        in_specs=[
            pl.BlockSpec((3 * GR, D), full),
            pl.BlockSpec((GR, D), full),
            pl.BlockSpec((3 * GR, 1), full),
            pl.BlockSpec((2, 2 * TOK, D), lambda i: (i, 0, 0)),
        ],
        out_specs=[
            pl.BlockSpec((3 * GR, 2 * TOK), lambda i: (0, i)),
            pl.BlockSpec((GR, 2 * TOK), lambda i: (0, i)),
        ],
        out_shape=[jax.ShapeDtypeStruct((3 * GR, S), BF16), jax.ShapeDtypeStruct((GR, S), BF16)],
        compiler_params=params(),
        cost_estimate=pl.CostEstimate(flops=2 * 4 * GR * D * S, bytes_accessed=35_000_000, transcendentals=0),
        name="project",
    )(wt, wo, bias, gathered)


def att_kernel(q_ref, k_ref, v_ref, do_ref, o_ref, dq_ref, dk_ref, dv_ref, db_ref, dk_acc, dv_acc):
    to_exp2 = SCALE * math.log2(math.e)
    k_t = k_ref[...]
    v_t = v_ref[...]
    k_n = k_t.T
    v_n = v_t.T
    db_q = jnp.zeros((DH, 1), F32)
    for i in reversed(range(S // BQ)):
        keys = (i + 1) * BQ
        cols = slice(i * BQ, keys)
        q = q_ref[:, cols]
        do = do_ref[:, cols]
        s = dot_nn(k_n[:keys], q)
        row = lax.broadcasted_iota(jnp.int32, (BQ, BQ), 0)
        col = lax.broadcasted_iota(jnp.int32, (BQ, BQ), 1)
        s_diag = jnp.where(row <= col, s[keys - BQ:], -1e30)
        s = jnp.concatenate([s[:keys - BQ], s_diag], axis=0) if i else s_diag
        m = jnp.max(s, axis=0, keepdims=True)
        p = jnp.exp2((s - m) * to_exp2)
        p = p * (1.0 / jnp.sum(p, axis=0, keepdims=True))
        p_low = p.astype(BF16)
        o_ref[:, cols] = dot_nn(v_t[:, :keys], p_low).astype(BF16)
        dp = dot_nn(v_n[:keys], do).astype(BF16).astype(F32)
        row_dot = jnp.sum(p * dp, axis=0, keepdims=True)
        ds = (p * (dp - row_dot) * SCALE).astype(BF16)
        dq = dot_nn(k_t[:, :keys], ds).astype(BF16)
        dq_ref[:, cols] = dq
        db_q += jnp.sum(dq.astype(F32), axis=1, keepdims=True)
        dk = dot_nt(q, ds)
        dv = dot_nt(do, p_low)
        if keys == S:
            dk_acc[...] = dk
            dv_acc[...] = dv
        else:
            dk_acc[:, :keys] += dk
            dv_acc[:, :keys] += dv
    dk = dk_acc[...].astype(BF16)
    dv = dv_acc[...].astype(BF16)
    dk_ref[...] = dk
    dv_ref[...] = dv
    db_k = jnp.sum(dk.astype(F32), axis=1, keepdims=True)
    db_v = jnp.sum(dv.astype(F32), axis=1, keepdims=True)
    for t, db in enumerate((db_q, db_k, db_v)):
        db_ref[t] = jnp.broadcast_to(db, (DH, 128))


def attention(qkv, do):
    spec = lambda off: pl.BlockSpec((DH, S), lambda h: (h + off, 0))
    return pl.pallas_call(
        att_kernel,
        grid=(GH,),
        in_specs=[spec(0), spec(GH), spec(2 * GH), spec(0)],
        out_specs=[spec(0)] * 4 + [pl.BlockSpec((3, DH, 128), lambda h: (0, h, 0))],
        out_shape=[jax.ShapeDtypeStruct((GR, S), BF16)] * 4 + [jax.ShapeDtypeStruct((3, GR, 128), F32)],
        scratch_shapes=[pltpu.VMEM((DH, S), F32)] * 2,
        compiler_params=params(),
        cost_estimate=pl.CostEstimate(flops=40_000_000_000, bytes_accessed=12_000_000, transcendentals=0),
        name="attention",
    )(qkv, qkv, qkv, do)


def collect_kernel(tbl, *refs):
    own_ref, peer_ref = refs[16:]
    for s in range(4):
        rows = pl.ds(pl.multiple_of(tbl[3 + s] * GR, GR), GR)
        for b in range(2):
            own_ref[rows, b * TOK:(b + 1) * TOK] = refs[s * 2 + b][...]
            peer_ref[rows, b * TOK:(b + 1) * TOK] = refs[8 + s * 2 + b][...]


def collect(tbl, pieces):
    own = pl.BlockSpec((GR, TOK), lambda i, t: (0, t[1]))
    peer = pl.BlockSpec((GR, TOK), lambda i, t: (0, t[2]))
    whole = pl.BlockSpec((CR, 2 * TOK), lambda i, t: (0, 0))
    return pl.pallas_call(
        collect_kernel,
        grid_spec=pltpu.PrefetchScalarGridSpec(
            num_scalar_prefetch=1, grid=(1,), in_specs=[own] * 8 + [peer] * 8, out_specs=[whole] * 2),
        out_shape=[jax.ShapeDtypeStruct((CR, 2 * TOK), BF16)] * 2,
        compiler_params=params(),
        cost_estimate=pl.CostEstimate(flops=1_000_000_000, bytes_accessed=3_000_000, transcendentals=0),
        name="collect",
    )(tbl, *pieces, *pieces)


BD = 256


def dw_kernel(tbl, x0, x1, *refs):
    pieces = refs[:8]
    out_ref, ex_ref, lhs_ref, sem = refs[-4:]

    @pl.when(pl.program_id(0) == 0)
    def _():
        copies = []
        for s in range(4):
            rows = pl.ds(pl.multiple_of(tbl[3 + s] * GR, GR), GR)
            for b in range(B):
                copies.append(pltpu.make_async_copy(
                    pieces[2 * s + b], lhs_ref.at[rows, pl.ds(b * S, S)], sem.at[2 * s + b]))
        for c in copies:
            c.start()
        for c in copies:
            c.wait()

    x = jnp.concatenate([x0[r] for r in range(NDEV)] + [x1[r] for r in range(NDEV)], axis=0)
    res = dot_nn(lhs_ref[...], x)
    out_ref[...] = res
    ex_ref[...] = res


def weight_grad(tbl, gathered, pieces, row_block, which, out_rows, prev=None):
    x_spec = pl.BlockSpec((NDEV, TOK, BD), lambda j, t: (0, which, j))
    anywhere = pl.BlockSpec(memory_space=pl.ANY)
    in_specs = [x_spec] * 2 + [anywhere] * 8
    args = [tbl, *gathered, *pieces]
    alias = {}
    if prev is not None:
        in_specs.append(anywhere)
        args.append(prev)
        alias = {len(args) - 1: 0}
    return pl.pallas_call(
        dw_kernel,
        grid_spec=pltpu.PrefetchScalarGridSpec(
            num_scalar_prefetch=1,
            grid=(D // BD,),
            in_specs=in_specs,
            out_specs=[
                pl.BlockSpec((CR, BD), lambda j, t: (2 * row_block + t[0], j)),
                pl.BlockSpec((CR, BD), lambda j, t: (0, j)),
            ],
            scratch_shapes=[pltpu.VMEM((CR, B * S), BF16), pltpu.SemaphoreType.DMA((8,))]),
        out_shape=[jax.ShapeDtypeStruct((out_rows, D), F32), jax.ShapeDtypeStruct((CR, D), F32)],
        input_output_aliases=alias,
        compiler_params=params(),
        cost_estimate=pl.CostEstimate(flops=2 * CR * D * B * S, bytes_accessed=75_000_000, transcendentals=0),
        name="weight_grad",
    )(*args)


def contract_kernel(first, tbl, here_ref, there_ref, w_ref, *refs):
    acc_ref = refs[-1]
    i = pl.program_id(0)

    @pl.when(i == 0)
    def _():
        acc_ref[...] = jnp.zeros_like(acc_ref) if first else refs[0][...]

    rows = pl.ds(pl.multiple_of((i % 4) * GR, GR), GR)
    act = jnp.where(i // 4 == tbl[0], here_ref[rows, :], there_ref[rows, :])
    acc_ref[...] += lax.dot_general(act, w_ref[...], (((0,), (0,)), ((), ())), preferred_element_type=F32)


def contract(tbl, here, there, weight, block, acc=None):
    whole = lambda shape: pl.BlockSpec(shape, lambda i, t: (0, 0))
    args = [tbl, here, there, weight] + ([] if acc is None else [acc])
    return pl.pallas_call(
        functools.partial(contract_kernel, acc is None),
        grid_spec=pltpu.PrefetchScalarGridSpec(
            num_scalar_prefetch=1,
            grid=(D // GR,),
            in_specs=[whole((CR, B * TOK))] * 2 + [pl.BlockSpec((GR, D), lambda i, t: (block * 8 + i, 0))]
            + ([] if acc is None else [whole((B * TOK, D))]),
            out_specs=whole((B * TOK, D))),
        out_shape=jax.ShapeDtypeStruct((B * TOK, D), F32),
        compiler_params=params(),
        cost_estimate=pl.CostEstimate(flops=2 * B * TOK * D * D, bytes_accessed=22_000_000, transcendentals=0),
        name="contract",
    )(*args)


def solution(mesh):
    def permute(a, bit):
        return lax.ppermute(a, "sp", [(i, i ^ bit) for i in range(NDEV)])

    def block(x_in, grad_y, ln_gain, ln_bias, w_qkv, b_qkv, w_out, b_out):
        me = lax.axis_index("sp")
        core = me % 2
        chip = me // 2
        group = lambda c: jnp.where(c < 4, c, 7 - c)
        groups = [group(chip), group(chip ^ 1), group(chip ^ 2), group(chip ^ 4)]
        tbl = jnp.stack([core, me, me ^ 1] + groups + [core]).astype(jnp.int32)
        mine = 4 * core + groups[0]

        x_float = x_in.astype(F32)
        centered = x_float - jnp.mean(x_float, axis=-1, keepdims=True)
        inv_std = lax.rsqrt(jnp.mean(centered * centered, axis=-1, keepdims=True) + LN_EPS)
        x_hat = centered * inv_std
        normed = (x_hat * ln_gain + ln_bias).astype(BF16)
        grad_b_out = jnp.sum(grad_y, axis=(0, 1), dtype=F32)

        w_rows = jnp.transpose(w_qkv, (1, 2, 3, 0)).reshape(3, 8, GR, D)
        wt = lax.dynamic_slice_in_dim(w_rows, mine, 1, axis=1).reshape(3 * GR, D)
        wo = lax.dynamic_slice_in_dim(w_out.reshape(8, GR, D), mine, 1, axis=0).reshape(GR, D)
        bias = lax.dynamic_slice_in_dim(b_qkv.reshape(3, 8, GR), mine, 1, axis=1).reshape(3 * GR, 1)

        local = [jnp.concatenate([normed[b], grad_y[b]], axis=0) for b in range(B)]
        g0 = lax.all_gather(local[0], "sp")
        second, g0 = lax.optimization_barrier((local[1], g0))
        g1 = lax.all_gather(second, "sp")
        gathered = [g0, g1]

        own = []
        for b in range(B):
            heads = project(wt, wo, bias, gathered[b])
            own.append(attention(*heads))
        db = own[0][4] + own[1][4]
        pieces = {}
        for name, idx in (("o", 0), ("v", 3), ("k", 2), ("q", 1)):
            got = []
            for s, bit in enumerate((0, 2, 4, 8)):
                for b in range(B):
                    got.append(own[b][idx] if s == 0 else permute(own[b][idx], bit))
            pieces[name] = got

        def tokens_of_mine(name, weight, block, acc=None):
            here, there = collect(tbl, pieces[name])
            there = permute(there, 1)
            return contract(tbl, here, there, weight, block, acc)

        proj_out = tokens_of_mine("o", w_out.reshape(D, D), 0).reshape(B, TOK, D) + b_out
        y_out = (x_float + proj_out).astype(BF16)

        def grad(name, t, prev=None):
            if name == "o":
                return weight_grad(tbl, gathered, pieces[name], 0, 1, D)
            return weight_grad(tbl, gathered, pieces[name], t, 0, 3 * D, prev)

        def put(buf, ex, t):
            ex = permute(ex, 1)
            return lax.dynamic_update_slice(buf, ex, (t * D + (1 - core) * CR, 0))

        gwo, ex_o = grad("o", 0)
        gwq, ex_v = grad("v", 2)
        gwq, ex_k = grad("k", 1, gwq)
        gwo = put(gwo, ex_o, 0)
        gwq = put(gwq, ex_v, 2)
        gwq, ex_q = grad("q", 0, gwq)
        gwq = put(gwq, ex_k, 1)
        gwq = put(gwq, ex_q, 0)

        flat_w = w_rows.reshape(3 * D, D)
        grad_normed = None
        for name, t in (("v", 2), ("k", 1), ("q", 0)):
            grad_normed = tokens_of_mine(name, flat_w, t, grad_normed)
        grad_normed = grad_normed.astype(BF16).astype(F32).reshape(B, TOK, D)
        grad_ln_gain = jnp.sum(grad_normed * x_hat, axis=(0, 1))
        grad_ln_bias = jnp.sum(grad_normed, axis=(0, 1))
        grad_hat = grad_normed * ln_gain
        mean_grad = jnp.mean(grad_hat, axis=-1, keepdims=True)
        mean_proj = jnp.mean(grad_hat * x_hat, axis=-1, keepdims=True)
        grad_x = (grad_y.astype(F32) + inv_std * (grad_hat - mean_grad - x_hat * mean_proj)).astype(BF16)

        db = jnp.where(chip < 4, db[:, :, 0], 0.0).reshape(3, 1, GR)
        db_all = lax.dynamic_update_slice(jnp.zeros((3, 8, GR), F32), db, (0, mine, 0)).reshape(3, D)
        small = jnp.concatenate([jnp.stack([grad_ln_gain, grad_ln_bias, grad_b_out]), db_all], axis=0)
        small = lax.psum(small, "sp")

        grad_w_qkv = jnp.transpose(gwq.reshape(3, NH, DH, D), (3, 0, 1, 2))
        return (y_out, grad_x, small[0], small[1], grad_w_qkv, small[3:6].reshape(3, NH, DH), gwo.reshape(NH, DH, D), small[2])

    seq = P(None, "sp", None)
    rep = P()

    return jax.shard_map(
        block, mesh=mesh, in_specs=(seq, seq, rep, rep, rep, rep, rep, rep),
        out_specs=(seq, seq, rep, rep, rep, rep, rep, rep), check_vma=False)
```

time: 2050 us -> 958 us (0.47)
  waiting for transfers between devices: 1160 us -> 392 us
  Pallas kernels: 0 us -> 432 us
  matrix products: 414 us -> 0 us
  local copies, waits for them, and re-layouts: 277 us -> 68.5 us
  blocking collectives: 130 us -> 0 us
    psum x3 -> x1, waiting for transfers between devices: 1110 us -> 64.4 us  [block(): small = lax.psum(small, 'sp')]
    pallas_call x0 -> x16, Pallas kernels: none -> 432 us  [the longest x4 204 us: weight_grad(): pl.pallas_call(dw_kernel, grid_spec=pltpu.PrefetchScalarGridSpec(num_scal...]
    dot_general x16 -> x0, matrix products: 336 us -> none  [the longest x2 67 us: head_attention_bwd(): jnp.einsum('crl,crf->clf', grad_s, qkv_head[0], preferred_element_type=jn...]
    ppermute x0 -> x32, waiting for transfers between devices: none -> 195 us  [permute(): return lax.ppermute(a, 'sp', [(i, i ^ bit) for i in range(NDEV)])]
    all_gather x0 -> x2, waiting for transfers between devices: none -> 133 us  [the longest x1 105 us: block(): g0 = lax.all_gather(local[0], 'sp')]
    all_to_all x2 -> x0, blocking collectives: 130 us -> none  [the longest x1 76.9 us: local_block(): grad_qkv_local = lax.all_to_all(grad_qkv_heads, 'sp', 3, 0, tiled=True)]
    unnamed x44 -> x31, local copies, waits for them, and re-layouts: 109 us -> 1.25 us
    sub x4 -> x0, matrix products: 78.2 us -> none  [head_probs(): return jax.nn.softmax(scores, axis=-1)]
  transfers between devices with their start and end apart: 5 -> 35, of which waited for: 3 -> 15; matrix products, arithmetic and copies ran while one was open for 14% -> 7% of each run, Pallas kernels for 0% -> 40%
where the time goes in v1:
time: 958 us; the launch traced here: 954 us
  Pallas kernels  432 us (45%)
  waiting for transfers between devices  392 us (41%)
  local copies, waits for them, and re-layouts  68.5 us (7%)
  starting transfers between devices  26.4 us (3%)
  other arithmetic  20.9 us (2%)
  between operations  14.3 us (1%)
    pallas_call x4, Pallas kernels, weight_grad(): pl.pallas_call(dw_kernel, grid_spec=pltpu.PrefetchScalarGridSpec(num_scal...  204 us
    ppermute x32, waiting for transfers between devices, permute(): return lax.ppermute(a, 'sp', [(i, i ^ bit) for i in range(NDEV)])  195 us
    all_gather x1, waiting for transfers between devices, block(): g0 = lax.all_gather(local[0], 'sp')  105 us
    pallas_call x2, Pallas kernels, attention(): pl.pallas_call(att_kernel, grid=(GH,), in_specs=[spec(0), spec(GH), spec(...  95.6 us
    psum x1, waiting for transfers between devices, block(): small = lax.psum(small, 'sp')  64.4 us
    pallas_call x4, Pallas kernels, contract(): pl.pallas_call(functools.partial(contract_kernel, acc is None), grid_spec...  62.8 us
    pallas_call x2, Pallas kernels, project(): pl.pallas_call(proj_kernel, grid=(NDEV // 2,), in_specs=[pl.BlockSpec((3...  54.4 us
    dynamic_update_slice x4, local copies, waits for them, and re-layouts, put(): return lax.dynamic_update_slice(buf, ex, (t * D + (1 - core) * CR, 0))  51.6 us
  transfers between devices with their start and end apart: 35, of which 15 were waited for; matrix products, arithmetic and copies ran while one was open for 7% of the time, Pallas kernels for 40%

profile of v1, /device:TPU:0, one launch (start us, length us, event | category | flops | bytes accessed | tf_op | source)
XLA Modules:
  0.0 953.9 jit_solution(963304801636931053)
XLA Ops:
  7.3 1.8 convert_reduce_fusion
  9.1 2.0 fusion.12
  15.4 105.4 %all-gather.5.cloned.1.call-done = bf16[4096,3072]{1,0:T(8,128)(2,1)} async-done(((bf16[256,3072]{1,0:T(8,128)(2,1)}), bf16[4096,3072]{1,0:T(8,128)(2,1)}) %all-gather.5.cloned.1.call-update) | async-done | bytes 25165840 | tf_op jit(solution)/shard_map/all_gather | solution.py:265
  122.1 3.2 dynamic-slice_bitcast_fusion.wo_ref
  125.3 6.9 constant_dynamic-slice_fusion.1
  132.2 27.3 %project.2 = (bf16[1152,2048]{1,0:T(8,128)(2,1)}, bf16[384,2048]{1,0:T(8,128)(2,1)}) custom-call(bf16[1152,3072]{1,0:T(8,128)(2,1)} %bitcast.67, bf16[384,3072]{1,0:T(8,128)(2,1)} %dynamic-slice_bitcast_fusion.wo_ref, f32[1152,1]{1,0:T(8,128)} %copy.26.bias_ref, bf16[16,256,3072]{2,1,0:T(8,128)(2,1)} %bitcast.54), custom_call_target="tpu_custom_call" | custom-call | flops 19327352832 | bytes 35000000 | tf_op jit(solution)/shard_map/project/pallas_call | solution.py:48
  159.5 47.9 %attention.2 = (bf16[384,2048]{1,0:T(8,128)(2,1)}, bf16[384,2048]{1,0:T(8,128)(2,1)}, bf16[384,2048]{1,0:T(8,128)(2,1)}, bf16[384,2048]{1,0:T(8,128)(2,1)}, f32[3,384,128]{2,1,0:T(8,128)}) custom-call(bf16[1152,2048]{1,0:T(8,128)(2,1)} %get-tuple-element.41.q_ref.k_ref.v_ref, bf16[1152,2048]{1,0:T(8,128)(2,1)} %get-tuple-element.41.q_ref.k_ref.v_ref, ...), custom_call_target="tpu_custom_call" | custom-call | flops 40000000000 | bytes 12000000 | tf_op jit(solution)/shard_map/attention/pallas_call | solution.py:116
  207.4 1.8 collective-permute-start.21
  209.3 1.5 collective-permute-start.23
  211.3 27.9 %all-gather.7.cloned.1.call-done = bf16[4096,3072]{1,0:T(8,128)(2,1)} async-done(((bf16[256,3072]{1,0:T(8,128)(2,1)}), bf16[4096,3072]{1,0:T(8,128)(2,1)}) %all-gather.7.cloned.1.call-update) | async-done | bytes 25165840 | tf_op jit(solution)/shard_map/all_gather | solution.py:267
  239.2 27.1 %project.3 = (bf16[1152,2048]{1,0:T(8,128)(2,1)}, bf16[384,2048]{1,0:T(8,128)(2,1)}) custom-call(bf16[1152,3072]{1,0:T(8,128)(2,1)} %bitcast.68, bf16[384,3072]{1,0:T(8,128)(2,1)} %dynamic-slice_bitcast_fusion.wo_ref, f32[1152,1]{1,0:T(8,128)} %copy.26.bias_ref, bf16[16,256,3072]{2,1,0:T(8,128)(2,1)} %bitcast.59), custom_call_target="tpu_custom_call" | custom-call | flops 19327352832 | bytes 35000000 | tf_op jit(solution)/shard_map/project/pallas_call | solution.py:48
  266.2 47.7 %attention.3 = (bf16[384,2048]{1,0:T(8,128)(2,1)}, bf16[384,2048]{1,0:T(8,128)(2,1)}, bf16[384,2048]{1,0:T(8,128)(2,1)}, bf16[384,2048]{1,0:T(8,128)(2,1)}, f32[3,384,128]{2,1,0:T(8,128)}) custom-call(bf16[1152,2048]{1,0:T(8,128)(2,1)} %get-tuple-element.45.q_ref.k_ref.v_ref, bf16[1152,2048]{1,0:T(8,128)(2,1)} %get-tuple-element.45.q_ref.k_ref.v_ref, ...), custom_call_target="tpu_custom_call" | custom-call | flops 40000000000 | bytes 12000000 | tf_op jit(solution)/shard_map/attention/pallas_call | solution.py:116
  314.3 2.5 collective-permute-start.24
  318.1 32.7 %collective-permute-done.22.refs_3_.refs_11_ = bf16[384,2048]{1,0:T(8,128)(2,1)} collective-permute-done((bf16[384,2048]{1,0:T(8,128)(2,1)}, bf16[384,2048]{1,0:T(8,128)(2,1)}, u32[]{:S(2)}, u32[]{:S(2)}) %collective-permute-start.22) | collective-permute-done | bytes 1572896 | tf_op jit(solution)/shard_map/ppermute | solution.py:241
  351.7 1.4 collective-permute-done.26.refs_7_.refs_15_
  353.2 51.4 %weight_grad.4 = (f32[9216,3072]{1,0:T(8,128)}, f32[1536,3072]{1,0:T(8,128)}) custom-call(s32[8]{0:T(128)} %stack.41.tbl, bf16[16,256,3072]{2,1,0:T(8,128)(2,1)} %bitcast.55, bf16[16,256,3072]{2,1,0:T(8,128)(2,1)} %bitcast.60, bf16[384,2048]{1,0:T(8,128)(2,1)} %get-tuple-element.58.refs_0_.refs_8_, bf16[384,2048]{1,0:T(8,128)(2,1)} %get-tuple-element.59.refs_1_.refs_9_, ...), custom_call_target="tpu_custom_call" | custom-call | flops 38654705664 | bytes 75000000 | tf_op jit(solution)/shard_map/weight_grad/pallas_call | solution.py:189
  408.0 34.2 %collective-permute-done.7.refs_2_.refs_10_ = bf16[384,2048]{1,0:T(8,128)(2,1)} collective-permute-done((bf16[384,2048]{1,0:T(8,128)(2,1)}, bf16[384,2048]{1,0:T(8,128)(2,1)}, u32[]{:S(2)}, u32[]{:S(2)}) %collective-permute-start.7) | collective-permute-done | bytes 1572896 | tf_op jit(solution)/shard_map/ppermute | solution.py:241
  442.5 33.4 %collective-permute-done.14.refs_2_.refs_10_ = bf16[384,2048]{1,0:T(8,128)(2,1)} collective-permute-done((bf16[384,2048]{1,0:T(8,128)(2,1)}, bf16[384,2048]{1,0:T(8,128)(2,1)}, u32[]{:S(2)}, u32[]{:S(2)}) %collective-permute-start.14) | collective-permute-done | bytes 1572896 | tf_op jit(solution)/shard_map/ppermute | solution.py:241
  476.8 1.7 collective-permute-start.1
  478.5 31.1 %collective-permute-done.refs_2_.refs_10_ = bf16[384,2048]{1,0:T(8,128)(2,1)} collective-permute-done((bf16[384,2048]{1,0:T(8,128)(2,1)}, bf16[384,2048]{1,0:T(8,128)(2,1)}, u32[]{:S(2)}, u32[]{:S(2)}) %collective-permute-start) | collective-permute-done | bytes 1572896 | tf_op jit(solution)/shard_map/ppermute | solution.py:241
  512.5 30.3 %collective-permute-done.1.refs_3_.refs_11_ = bf16[384,2048]{1,0:T(8,128)(2,1)} collective-permute-done((bf16[384,2048]{1,0:T(8,128)(2,1)}, bf16[384,2048]{1,0:T(8,128)(2,1)}, u32[]{:S(2)}, u32[]{:S(2)}) %collective-permute-start.1) | collective-permute-done | bytes 1572896 | tf_op jit(solution)/shard_map/ppermute | solution.py:241
  543.7 1.6 collective-permute-done.3.refs_5_.refs_13_
  545.6 1.9 collective-permute-done.5.refs_7_.refs_15_
  548.7 50.9 %weight_grad.7 = (f32[3072,3072]{1,0:T(8,128)}, f32[1536,3072]{1,0:T(8,128)}) custom-call(s32[8]{0:T(128)} %stack.41.tbl, bf16[16,256,3072]{2,1,0:T(8,128)(2,1)} %bitcast.56, bf16[16,256,3072]{2,1,0:T(8,128)(2,1)} %bitcast.61, bf16[384,2048]{1,0:T(8,128)(2,1)} %get-tuple-element.43.refs_0_.refs_8_, bf16[384,2048]{1,0:T(8,128)(2,1)} %get-tuple-element.47.refs_1_.refs_9_, ...), custom_call_target="tpu_custom_call" | custom-call | flops 38654705664 | bytes 75000000 | tf_op jit(solution)/shard_map/weight_grad/pallas_call | solution.py:189
  599.6 1.5 collective-permute-start.9
  603.1 11.8 %collective-permute-done.19.refs_7_.refs_15_ = bf16[384,2048]{1,0:T(8,128)(2,1)} collective-permute-done((bf16[384,2048]{1,0:T(8,128)(2,1)}, bf16[384,2048]{1,0:T(8,128)(2,1)}, u32[]{:S(2)}, u32[]{:S(2)}) %collective-permute-start.19) | collective-permute-done | bytes 1572896 | tf_op jit(solution)/shard_map/ppermute | solution.py:241
  614.9 1.7 collective-permute-start.10
  617.6 50.9 %weight_grad.5 = (f32[9216,3072]{1,0:T(8,128)}, f32[1536,3072]{1,0:T(8,128)}) custom-call(s32[8]{0:T(128)} %stack.41.tbl, bf16[16,256,3072]{2,1,0:T(8,128)(2,1)} %bitcast.57, bf16[16,256,3072]{2,1,0:T(8,128)(2,1)} %bitcast.62, bf16[384,2048]{1,0:T(8,128)(2,1)} %get-tuple-element.54.refs_0_.refs_8_, ...), custom_call_target="tpu_custom_call", output_to_operand_aliasing={{0}: (11, {})} | custom-call | flops 38654705664 | bytes 75000000 | tf_op jit(solution)/shard_map/weight_grad/pallas_call | solution.py:189
  668.5 12.9 %constant_dynamic-update-slice_fusion.3.refs_8_ = f32[9216,3072]{1,0:T(8,128)} fusion(f32[9216,3072]{1,0:T(8,128)} %get-tuple-element.65, f32[1536,3072]{1,0:T(8,128)} %collective-permute-done.28, s32[]{:T(128)S(6)} %select_n.69), kind=kLoop, calls=%fused_computation.36 | loop fusion | bytes 37748740 | tf_op jit(solution)/shard_map/dynamic_update_slice | solution.py:298
  681.9 51.1 %weight_grad.6 = (f32[9216,3072]{1,0:T(8,128)}, f32[1536,3072]{1,0:T(8,128)}) custom-call(s32[8]{0:T(128)} %stack.41.tbl, bf16[16,256,3072]{2,1,0:T(8,128)(2,1)} %bitcast.58, bf16[16,256,3072]{2,1,0:T(8,128)(2,1)} %bitcast.63, bf16[384,2048]{1,0:T(8,128)(2,1)} %get-tuple-element.50.refs_0_.refs_8_, ...), custom_call_target="tpu_custom_call", output_to_operand_aliasing={{0}: (11, {})} | custom-call | flops 38654705664 | bytes 75000000 | tf_op jit(solution)/shard_map/weight_grad/pallas_call | solution.py:189
  733.1 3.6 collect.7
  737.2 3.6 collect.6
  740.9 1.5 fusion.16
  743.1 3.6 collect.5
  746.7 3.6 collect.4
  750.3 14.7 %collective-permute-done.27.there_ref = bf16[1536,256]{1,0:T(8,128)(2,1)} collective-permute-done((bf16[1536,256]{1,0:T(8,128)(2,1)}, bf16[1536,256]{1,0:T(8,128)(2,1)}, u32[]{:S(2)}, u32[]{:S(2)}) %collective-permute-start.27) | collective-permute-done | bytes 786464 | tf_op jit(solution)/shard_map/ppermute | solution.py:241
  765.1 15.2 %contract.5.refs_0_ = f32[256,3072]{1,0:T(8,128)} custom-call(s32[8]{0:T(128)} %stack.41.tbl, bf16[1536,256]{1,0:T(8,128)(2,1)} %get-tuple-element.60.here_ref, bf16[1536,256]{1,0:T(8,128)(2,1)} %collective-permute-done.27.there_ref, bf16[9216,3072]{1,0:T(8,128)(2,1)} %bitcast.51), custom_call_target="tpu_custom_call" | custom-call | flops 4831838208 | bytes 22000000 | tf_op jit(solution)/shard_map/contract/pallas_call | solution.py:224
  780.7 16.2 %contract.6.refs_0_ = f32[256,3072]{1,0:T(8,128)} custom-call(s32[8]{0:T(128)} %stack.41.tbl, bf16[1536,256]{1,0:T(8,128)(2,1)} %get-tuple-element.56.here_ref, bf16[1536,256]{1,0:T(8,128)(2,1)} %collective-permute-done.20.there_ref, bf16[9216,3072]{1,0:T(8,128)(2,1)} %bitcast.52, f32[256,3072]{1,0:T(8,128)} %contract.5.refs_0_), custom_call_target="tpu_custom_call" | custom-call | flops 4831838208 | bytes 22000000 | tf_op jit(solution)/shard_map/contract/pallas_call | solution.py:224
  796.9 16.2 %contract.7 = f32[256,3072]{1,0:T(8,128)} custom-call(s32[8]{0:T(128)} %stack.41.tbl, bf16[1536,256]{1,0:T(8,128)(2,1)} %get-tuple-element.52.here_ref, bf16[1536,256]{1,0:T(8,128)(2,1)} %collective-permute-done.13.there_ref, bf16[9216,3072]{1,0:T(8,128)(2,1)} %bitcast.53, f32[256,3072]{1,0:T(8,128)} %contract.6.refs_0_), custom_call_target="tpu_custom_call" | custom-call | flops 4831838208 | bytes 22000000 | tf_op jit(solution)/shard_map/contract/pallas_call | solution.py:224
  813.1 3.2 convert_reduce_fusion.2
  816.3 1.7 fusion.11
  819.2 15.2 %contract.4 = f32[256,3072]{1,0:T(8,128)} custom-call(s32[8]{0:T(128)} %stack.41.tbl, bf16[1536,256]{1,0:T(8,128)(2,1)} %get-tuple-element.48.here_ref, bf16[1536,256]{1,0:T(8,128)(2,1)} %collective-permute-done.6.there_ref, bf16[3072,3072]{1,0:T(8,128)(2,1)} %bitcast.66), custom_call_target="tpu_custom_call" | custom-call | flops 4831838208 | bytes 22000000 | tf_op jit(solution)/shard_map/contract/pallas_call | solution.py:224
  834.5 5.5 convert_reduce_fusion.1
  840.7 64.4 %all-reduce.2.cloned.1.call-done = f32[6,3072]{1,0:T(8,128)} async-done(((f32[6,3072]{1,0:T(8,128)}), f32[6,3072]{1,0:T(8,128)}) %all-reduce.2.cloned.1.call-update) | async-done | bytes 73744 | tf_op jit(solution)/shard_map/psum | solution.py:324
  906.7 1.7 fusion.17
  908.4 12.9 %constant_dynamic-update-slice_fusion.2 = f32[9216,3072]{1,0:T(8,128)} fusion(f32[9216,3072]{1,0:T(8,128)} %get-tuple-element.67, f32[1536,3072]{1,0:T(8,128)} %collective-permute-done.29, s32[]{:T(128)S(6)} %select_n.70), kind=kLoop, calls=%fused_computation.35 | loop fusion | bytes 37748740 | tf_op jit(solution)/shard_map/dynamic_update_slice | solution.py:298
  921.3 12.9 %constant_dynamic-update-slice_fusion = f32[3072,3072]{1,0:T(8,128)} fusion(f32[3072,3072]{1,0:T(8,128)} %get-tuple-element.70, f32[1536,3072]{1,0:T(8,128)} %collective-permute-done.31, s32[]{:T(128)S(6)} %select_n.72), kind=kLoop, calls=%fused_computation.33 | loop fusion | bytes 37748740 | tf_op jit(solution)/shard_map/dynamic_update_slice | solution.py:298
  934.3 12.9 %constant_dynamic-update-slice_fusion.1 = f32[9216,3072]{1,0:T(8,128)} fusion(f32[9216,3072]{1,0:T(8,128)} %constant_dynamic-update-slice_fusion.2, f32[1536,3072]{1,0:T(8,128)} %collective-permute-done.30, s32[]{:T(128)S(6)} %select_n.71), kind=kLoop, calls=%fused_computation.34 | loop fusion | bytes 37748740 | tf_op jit(solution)/shard_map/dynamic_update_slice | solution.py:298
  (103 shorter events, 27.3 us)
Async XLA Ops:
  7.2 4.5 copy-start
  7.2 4.5 copy-start.5
  7.2 4.5 copy-start.14
  7.2 5.3 copy-start.3
  7.2 113.6 %all-gather.5.cloned.1.call-start = ((), (), s32[]{:S(2)}) async-start(), calls=%async_computation.1 | async-start | bytes 26738688 | tf_op jit(solution)/shard_map/all_gather | solution.py:265
  9.1 2.0 copy-start.10
  14.0 106.9 %copy-start.8 = (f32[3,32,96]{2,1,0:T(8,128)S(1)}, f32[3,32,96]{2,1,0:T(8,128)}, u32[]{:S(2)}) copy-start(f32[3,32,96]{2,1,0:T(8,128)} %param.13) | copy-start | bytes 110596
  14.0 225.1 %all-gather.7.cloned.1.call-start = ((), (), s32[]{:S(2)}) async-start(), calls=%async_computation.2 | async-start | bytes 26738688 | tf_op jit(solution)/shard_map/all_gather | solution.py:267
  120.8 784.3 %all-reduce.2.cloned.1.call-start = ((), (), s32[]{:S(2)}) async-start(), calls=%async_computation | async-start | bytes 196608 | tf_op jit(solution)/shard_map/psum | solution.py:324
  207.4 109.4 %collective-permute-start.21 = (bf16[384,2048]{1,0:T(8,128)(2,1)}, bf16[384,2048]{1,0:T(8,128)(2,1)}, u32[]{:S(2)}, u32[]{:S(2)}) collective-permute-start(bf16[384,2048]{1,0:T(8,128)(2,1)} %get-tuple-element.58.refs_0_.refs_8_), channel_id=1, source_target_pairs={{0,2},{1,3},{2,0},{3,1},{4,6},{5,7},{6,4},{7,5},{8,10},{9,11},{10,... | collective-permute-start | bytes 4718600 | tf_op jit(solution)/shard_map/ppermute | solution.py:241
  209.3 108.8 %collective-permute-start.23 = (bf16[384,2048]{1,0:T(8,128)(2,1)}, bf16[384,2048]{1,0:T(8,128)(2,1)}, u32[]{:S(2)}, u32[]{:S(2)}) collective-permute-start(bf16[384,2048]{1,0:T(8,128)(2,1)} %get-tuple-element.58.refs_0_.refs_8_), channel_id=1, source_target_pairs={{0,4},{1,5},{2,6},{3,7},{4,0},{5,1},{6,2},{7,3},{8,12},{9,13},{10,... | collective-permute-start | bytes 4718600 | tf_op jit(solution)/shard_map/ppermute | solution.py:241
  210.7 107.4 %collective-permute-start.25 = (bf16[384,2048]{1,0:T(8,128)(2,1)}, bf16[384,2048]{1,0:T(8,128)(2,1)}, u32[]{:S(2)}, u32[]{:S(2)}) collective-permute-start(bf16[384,2048]{1,0:T(8,128)(2,1)} %get-tuple-element.58.refs_0_.refs_8_), channel_id=1, source_target_pairs={{0,8},{1,9},{2,10},{3,11},{4,12},{5,13},{6,14},{7,15},{8,0},{9,1},... | collective-permute-start | bytes 4718600 | tf_op jit(solution)/shard_map/ppermute | solution.py:241
  314.0 36.9 %collective-permute-start.22 = (bf16[384,2048]{1,0:T(8,128)(2,1)}, bf16[384,2048]{1,0:T(8,128)(2,1)}, u32[]{:S(2)}, u32[]{:S(2)}) collective-permute-start(bf16[384,2048]{1,0:T(8,128)(2,1)} %get-tuple-element.59.refs_1_.refs_9_), channel_id=1, source_target_pairs={{0,2},{1,3},{2,0},{3,1},{4,6},{5,7},{6,4},{7,5},{8,10},{9,11},{10,... | collective-permute-start | bytes 4718600 | tf_op jit(solution)/shard_map/ppermute | solution.py:241
  314.3 37.4 %collective-permute-start.24 = (bf16[384,2048]{1,0:T(8,128)(2,1)}, bf16[384,2048]{1,0:T(8,128)(2,1)}, u32[]{:S(2)}, u32[]{:S(2)}) collective-permute-start(bf16[384,2048]{1,0:T(8,128)(2,1)} %get-tuple-element.59.refs_1_.refs_9_), channel_id=1, source_target_pairs={{0,4},{1,5},{2,6},{3,7},{4,0},{5,1},{6,2},{7,3},{8,12},{9,13},{10,... | collective-permute-start | bytes 4718600 | tf_op jit(solution)/shard_map/ppermute | solution.py:241
  316.9 36.3 %collective-permute-start.26 = (bf16[384,2048]{1,0:T(8,128)(2,1)}, bf16[384,2048]{1,0:T(8,128)(2,1)}, u32[]{:S(2)}, u32[]{:S(2)}) collective-permute-start(bf16[384,2048]{1,0:T(8,128)(2,1)} %get-tuple-element.59.refs_1_.refs_9_), channel_id=1, source_target_pairs={{0,8},{1,9},{2,10},{3,11},{4,12},{5,13},{6,14},{7,15},{8,0},{9,1},... | collective-permute-start | bytes 4718600 | tf_op jit(solution)/shard_map/ppermute | solution.py:241
  404.5 212.1 %collective-permute-start.28 = (f32[1536,3072]{1,0:T(8,128)}, f32[1536,3072]{1,0:T(8,128)}, u32[]{:S(2)}, u32[]{:S(2)}) collective-permute-start(f32[1536,3072]{1,0:T(8,128)} %get-tuple-element.66), channel_id=1, source_target_pairs={{0,1},{1,0},{2,3},{3,2},{4,5},{5,4},{6,7},{7,6},{8,9},{9,8},{10,11... | collective-permute-start | bytes 56623112 | tf_op jit(solution)/shard_map/ppermute | solution.py:241
  404.6 37.6 %collective-permute-start.7 = (bf16[384,2048]{1,0:T(8,128)(2,1)}, bf16[384,2048]{1,0:T(8,128)(2,1)}, u32[]{:S(2)}, u32[]{:S(2)}) collective-permute-start(bf16[384,2048]{1,0:T(8,128)(2,1)} %get-tuple-element.50.refs_0_.refs_8_), channel_id=1, source_target_pairs={{0,2},{1,3},{2,0},{3,1},{4,6},{5,7},{6,4},{7,5},{8,10},{9,11},{10,... | collective-permute-start | bytes 4718600 | tf_op jit(solution)/shard_map/ppermute | solution.py:241
  405.5 70.4 %collective-permute-start.14 = (bf16[384,2048]{1,0:T(8,128)(2,1)}, bf16[384,2048]{1,0:T(8,128)(2,1)}, u32[]{:S(2)}, u32[]{:S(2)}) collective-permute-start(bf16[384,2048]{1,0:T(8,128)(2,1)} %get-tuple-element.54.refs_0_.refs_8_), channel_id=1, source_target_pairs={{0,2},{1,3},{2,0},{3,1},{4,6},{5,7},{6,4},{7,5},{8,10},{9,11},{10,... | collective-permute-start | bytes 4718600 | tf_op jit(solution)/shard_map/ppermute | solution.py:241
  406.7 70.2 %collective-permute-start.16 = (bf16[384,2048]{1,0:T(8,128)(2,1)}, bf16[384,2048]{1,0:T(8,128)(2,1)}, u32[]{:S(2)}, u32[]{:S(2)}) collective-permute-start(bf16[384,2048]{1,0:T(8,128)(2,1)} %get-tuple-element.54.refs_0_.refs_8_), channel_id=1, source_target_pairs={{0,4},{1,5},{2,6},{3,7},{4,0},{5,1},{6,2},{7,3},{8,12},{9,13},{10,... | collective-permute-start | bytes 4718600 | tf_op jit(solution)/shard_map/ppermute | solution.py:241
  406.9 102.7 %collective-permute-start = (bf16[384,2048]{1,0:T(8,128)(2,1)}, bf16[384,2048]{1,0:T(8,128)(2,1)}, u32[]{:S(2)}, u32[]{:S(2)}) collective-permute-start(bf16[384,2048]{1,0:T(8,128)(2,1)} %get-tuple-element.43.refs_0_.refs_8_), channel_id=1, source_target_pairs={{0,2},{1,3},{2,0},{3,1},{4,6},{5,7},{6,4},{7,5},{8,10},{9,11},{10,... | collective-permute-start | bytes 4718600 | tf_op jit(solution)/shard_map/ppermute | solution.py:241
  442.2 67.7 %collective-permute-start.2 = (bf16[384,2048]{1,0:T(8,128)(2,1)}, bf16[384,2048]{1,0:T(8,128)(2,1)}, u32[]{:S(2)}, u32[]{:S(2)}) collective-permute-start(bf16[384,2048]{1,0:T(8,128)(2,1)} %get-tuple-element.43.refs_0_.refs_8_), channel_id=1, source_target_pairs={{0,4},{1,5},{2,6},{3,7},{4,0},{5,1},{6,2},{7,3},{8,12},{9,13},{10,... | collective-permute-start | bytes 4718600 | tf_op jit(solution)/shard_map/ppermute | solution.py:241
  475.9 35.7 %collective-permute-start.4 = (bf16[384,2048]{1,0:T(8,128)(2,1)}, bf16[384,2048]{1,0:T(8,128)(2,1)}, u32[]{:S(2)}, u32[]{:S(2)}) collective-permute-start(bf16[384,2048]{1,0:T(8,128)(2,1)} %get-tuple-element.43.refs_0_.refs_8_), channel_id=1, source_target_pairs={{0,8},{1,9},{2,10},{3,11},{4,12},{5,13},{6,14},{7,15},{8,0},{9,1},... | collective-permute-start | bytes 4718600 | tf_op jit(solution)/shard_map/ppermute | solution.py:241
  476.8 66.0 %collective-permute-start.1 = (bf16[384,2048]{1,0:T(8,128)(2,1)}, bf16[384,2048]{1,0:T(8,128)(2,1)}, u32[]{:S(2)}, u32[]{:S(2)}) collective-permute-start(bf16[384,2048]{1,0:T(8,128)(2,1)} %get-tuple-element.47.refs_1_.refs_9_), channel_id=1, source_target_pairs={{0,2},{1,3},{2,0},{3,1},{4,6},{5,7},{6,4},{7,5},{8,10},{9,11},{10,... | collective-permute-start | bytes 4718600 | tf_op jit(solution)/shard_map/ppermute | solution.py:241
  509.6 35.7 %collective-permute-start.3 = (bf16[384,2048]{1,0:T(8,128)(2,1)}, bf16[384,2048]{1,0:T(8,128)(2,1)}, u32[]{:S(2)}, u32[]{:S(2)}) collective-permute-start(bf16[384,2048]{1,0:T(8,128)(2,1)} %get-tuple-element.47.refs_1_.refs_9_), channel_id=1, source_target_pairs={{0,4},{1,5},{2,6},{3,7},{4,0},{5,1},{6,2},{7,3},{8,12},{9,13},{10,... | collective-permute-start | bytes 4718600 | tf_op jit(solution)/shard_map/ppermute | solution.py:241
  509.9 37.6 %collective-permute-start.5 = (bf16[384,2048]{1,0:T(8,128)(2,1)}, bf16[384,2048]{1,0:T(8,128)(2,1)}, u32[]{:S(2)}, u32[]{:S(2)}) collective-permute-start(bf16[384,2048]{1,0:T(8,128)(2,1)} %get-tuple-element.47.refs_1_.refs_9_), channel_id=1, source_target_pairs={{0,8},{1,9},{2,10},{3,11},{4,12},{5,13},{6,14},{7,15},{8,0},{9,1},... | collective-permute-start | bytes 4718600 | tf_op jit(solution)/shard_map/ppermute | solution.py:241
  511.6 88.0 %collective-permute-start.18 = (bf16[384,2048]{1,0:T(8,128)(2,1)}, bf16[384,2048]{1,0:T(8,128)(2,1)}, u32[]{:S(2)}, u32[]{:S(2)}) collective-permute-start(bf16[384,2048]{1,0:T(8,128)(2,1)} %get-tuple-element.54.refs_0_.refs_8_), channel_id=1, source_target_pairs={{0,8},{1,9},{2,10},{3,11},{4,12},{5,13},{6,14},{7,15},{8,0},{9,1},... | collective-permute-start | bytes 4718600 | tf_op jit(solution)/shard_map/ppermute | solution.py:241
  542.8 58.3 %collective-permute-start.15 = (bf16[384,2048]{1,0:T(8,128)(2,1)}, bf16[384,2048]{1,0:T(8,128)(2,1)}, u32[]{:S(2)}, u32[]{:S(2)}) collective-permute-start(bf16[384,2048]{1,0:T(8,128)(2,1)} %get-tuple-element.55.refs_1_.refs_9_), channel_id=1, source_target_pairs={{0,2},{1,3},{2,0},{3,1},{4,6},{5,7},{6,4},{7,5},{8,10},{9,11},{10,... | collective-permute-start | bytes 4718600 | tf_op jit(solution)/shard_map/ppermute | solution.py:241
  545.3 56.9 %collective-permute-start.17 = (bf16[384,2048]{1,0:T(8,128)(2,1)}, bf16[384,2048]{1,0:T(8,128)(2,1)}, u32[]{:S(2)}, u32[]{:S(2)}) collective-permute-start(bf16[384,2048]{1,0:T(8,128)(2,1)} %get-tuple-element.55.refs_1_.refs_9_), channel_id=1, source_target_pairs={{0,4},{1,5},{2,6},{3,7},{4,0},{5,1},{6,2},{7,3},{8,12},{9,13},{10,... | collective-permute-start | bytes 4718600 | tf_op jit(solution)/shard_map/ppermute | solution.py:241
  547.5 67.4 %collective-permute-start.19 = (bf16[384,2048]{1,0:T(8,128)(2,1)}, bf16[384,2048]{1,0:T(8,128)(2,1)}, u32[]{:S(2)}, u32[]{:S(2)}) collective-permute-start(bf16[384,2048]{1,0:T(8,128)(2,1)} %get-tuple-element.55.refs_1_.refs_9_), channel_id=1, source_target_pairs={{0,8},{1,9},{2,10},{3,11},{4,12},{5,13},{6,14},{7,15},{8,0},{9,1},... | collective-permute-start | bytes 4718600 | tf_op jit(solution)/shard_map/ppermute | solution.py:241
  599.6 81.8 %collective-permute-start.9 = (bf16[384,2048]{1,0:T(8,128)(2,1)}, bf16[384,2048]{1,0:T(8,128)(2,1)}, u32[]{:S(2)}, u32[]{:S(2)}) collective-permute-start(bf16[384,2048]{1,0:T(8,128)(2,1)} %get-tuple-element.50.refs_0_.refs_8_), channel_id=1, source_target_pairs={{0,4},{1,5},{2,6},{3,7},{4,0},{5,1},{6,2},{7,3},{8,12},{9,13},{10,... | collective-permute-start | bytes 4718600 | tf_op jit(solution)/shard_map/ppermute | solution.py:241
  601.1 80.3 %collective-permute-start.11 = (bf16[384,2048]{1,0:T(8,128)(2,1)}, bf16[384,2048]{1,0:T(8,128)(2,1)}, u32[]{:S(2)}, u32[]{:S(2)}) collective-permute-start(bf16[384,2048]{1,0:T(8,128)(2,1)} %get-tuple-element.50.refs_0_.refs_8_), channel_id=1, source_target_pairs={{0,8},{1,9},{2,10},{3,11},{4,12},{5,13},{6,14},{7,15},{8,0},{9,1},... | collective-permute-start | bytes 4718600 | tf_op jit(solution)/shard_map/ppermute | solution.py:241
  602.2 79.7 %collective-permute-start.8 = (bf16[384,2048]{1,0:T(8,128)(2,1)}, bf16[384,2048]{1,0:T(8,128)(2,1)}, u32[]{:S(2)}, u32[]{:S(2)}) collective-permute-start(bf16[384,2048]{1,0:T(8,128)(2,1)} %get-tuple-element.51.refs_1_.refs_9_), channel_id=1, source_target_pairs={{0,2},{1,3},{2,0},{3,1},{4,6},{5,7},{6,4},{7,5},{8,10},{9,11},{10,... | collective-permute-start | bytes 4718600 | tf_op jit(solution)/shard_map/ppermute | solution.py:241
  614.9 67.0 %collective-permute-start.10 = (bf16[384,2048]{1,0:T(8,128)(2,1)}, bf16[384,2048]{1,0:T(8,128)(2,1)}, u32[]{:S(2)}, u32[]{:S(2)}) collective-permute-start(bf16[384,2048]{1,0:T(8,128)(2,1)} %get-tuple-element.51.refs_1_.refs_9_), channel_id=1, source_target_pairs={{0,4},{1,5},{2,6},{3,7},{4,0},{5,1},{6,2},{7,3},{8,12},{9,13},{10,... | collective-permute-start | bytes 4718600 | tf_op jit(solution)/shard_map/ppermute | solution.py:241
  616.7 65.3 %collective-permute-start.12 = (bf16[384,2048]{1,0:T(8,128)(2,1)}, bf16[384,2048]{1,0:T(8,128)(2,1)}, u32[]{:S(2)}, u32[]{:S(2)}) collective-permute-start(bf16[384,2048]{1,0:T(8,128)(2,1)} %get-tuple-element.51.refs_1_.refs_9_), channel_id=1, source_target_pairs={{0,8},{1,9},{2,10},{3,11},{4,12},{5,13},{6,14},{7,15},{8,0},{9,1},... | collective-permute-start | bytes 4718600 | tf_op jit(solution)/shard_map/ppermute | solution.py:241
  681.4 227.0 %collective-permute-start.29 = (f32[1536,3072]{1,0:T(8,128)}, f32[1536,3072]{1,0:T(8,128)}, u32[]{:S(2)}, u32[]{:S(2)}) collective-permute-start(f32[1536,3072]{1,0:T(8,128)} %get-tuple-element.68), channel_id=1, source_target_pairs={{0,1},{1,0},{2,3},{3,2},{4,5},{5,4},{6,7},{7,6},{8,9},{9,8},{10,11... | collective-permute-start | bytes 56623112 | tf_op jit(solution)/shard_map/ppermute | solution.py:241
  681.4 239.9 %collective-permute-start.31 = (f32[1536,3072]{1,0:T(8,128)}, f32[1536,3072]{1,0:T(8,128)}, u32[]{:S(2)}, u32[]{:S(2)}) collective-permute-start(f32[1536,3072]{1,0:T(8,128)} %get-tuple-element.71), channel_id=1, source_target_pairs={{0,1},{1,0},{2,3},{3,2},{4,5},{5,4},{6,7},{7,6},{8,9},{9,8},{10,11... | collective-permute-start | bytes 56623112 | tf_op jit(solution)/shard_map/ppermute | solution.py:241
  733.0 201.2 %collective-permute-start.30 = (f32[1536,3072]{1,0:T(8,128)}, f32[1536,3072]{1,0:T(8,128)}, u32[]{:S(2)}, u32[]{:S(2)}) collective-permute-start(f32[1536,3072]{1,0:T(8,128)} %get-tuple-element.69), channel_id=1, source_target_pairs={{0,1},{1,0},{2,3},{3,2},{4,5},{5,4},{6,7},{7,6},{8,9},{9,8},{10,11... | collective-permute-start | bytes 56623112 | tf_op jit(solution)/shard_map/ppermute | solution.py:241
  736.7 28.3 %collective-permute-start.27 = (bf16[1536,256]{1,0:T(8,128)(2,1)}, bf16[1536,256]{1,0:T(8,128)(2,1)}, u32[]{:S(2)}, u32[]{:S(2)}) collective-permute-start(bf16[1536,256]{1,0:T(8,128)(2,1)} %get-tuple-element.61), channel_id=1, source_target_pairs={{0,1},{1,0},{2,3},{3,2},{4,5},{5,4},{6,7},{7,6},{8,9},{9,8},{10,11... | collective-permute-start | bytes 2359304 | tf_op jit(solution)/shard_map/ppermute | solution.py:241
  740.8 39.5 %collective-permute-start.20 = (bf16[1536,256]{1,0:T(8,128)(2,1)}, bf16[1536,256]{1,0:T(8,128)(2,1)}, u32[]{:S(2)}, u32[]{:S(2)}) collective-permute-start(bf16[1536,256]{1,0:T(8,128)(2,1)} %get-tuple-element.57), channel_id=1, source_target_pairs={{0,1},{1,0},{2,3},{3,2},{4,5},{5,4},{6,7},{7,6},{8,9},{9,8},{10,11... | collective-permute-start | bytes 2359304 | tf_op jit(solution)/shard_map/ppermute | solution.py:241
  765.0 31.9 %collective-permute-start.13 = (bf16[1536,256]{1,0:T(8,128)(2,1)}, bf16[1536,256]{1,0:T(8,128)(2,1)}, u32[]{:S(2)}, u32[]{:S(2)}) collective-permute-start(bf16[1536,256]{1,0:T(8,128)(2,1)} %get-tuple-element.53), channel_id=1, source_target_pairs={{0,1},{1,0},{2,3},{3,2},{4,5},{5,4},{6,7},{7,6},{8,9},{9,8},{10,11... | collective-permute-start | bytes 2359304 | tf_op jit(solution)/shard_map/ppermute | solution.py:241
  780.3 38.9 %collective-permute-start.6 = (bf16[1536,256]{1,0:T(8,128)(2,1)}, bf16[1536,256]{1,0:T(8,128)(2,1)}, u32[]{:S(2)}, u32[]{:S(2)}) collective-permute-start(bf16[1536,256]{1,0:T(8,128)(2,1)} %get-tuple-element.49), channel_id=1, source_target_pairs={{0,1},{1,0},{2,3},{3,2},{4,5},{5,4},{6,7},{7,6},{8,9},{9,8},{10,11... | collective-permute-start | bytes 2359304 | tf_op jit(solution)/shard_map/ppermute | solution.py:241
  813.1 3.2 copy-start.1
  813.1 3.2 copy-start.6
  813.1 3.2 copy-start.11
  813.1 3.2 copy-start.13
  834.4 5.5 copy-start.4
  834.4 5.6 copy-start.7
  834.4 5.6 copy-start.9
  (2 other events, 2.3 us)
Sparse Core Ops, SparseCore 0:
  14.2 106.5 all-gather.4
  123.0 116.0 all-gather.6
  840.8 64.2 all-reduce.1

commit v2 on v0

v2 whole, which is shorter than its diff:
```python
import functools
import math

import jax
import jax.numpy as jnp
from jax import lax
from jax.experimental import pallas as pl
from jax.experimental.pallas import tpu as pltpu
from jax.sharding import PartitionSpec as P


LN_EPS = 1e-5
F32 = jnp.float32
BF16 = jnp.bfloat16
VMEM_LIMIT = 64 * 1024 * 1024 - 65536

B, S, D, NH, DH = 2, 2048, 3072, 32, 96
NDEV = 16
TOK = S // NDEV
GH = 4
GR = GH * DH
CR = 4 * GR
SCALE = DH ** -0.5
BQ = 512
LANES = 128


def dot_nt(a, b):
    return lax.dot_general(a, b, (((1,), (1,)), ((), ())), preferred_element_type=F32)


def dot_nn(a, b):
    return jnp.dot(a, b, preferred_element_type=F32)


def params(**kw):
    return pltpu.CompilerParams(vmem_limit_bytes=VMEM_LIMIT, **kw)


def cost(flops, moved):
    return pl.CostEstimate(flops=int(flops), bytes_accessed=int(moved), transcendentals=0)


ROWS = dict(axis=0, keepdims=True)
LAST_DIM = dict(axis=-1, keepdims=True)


def normalize(x):
    centered = x - jnp.mean(x, **LAST_DIM)
    inv_std = lax.rsqrt(jnp.mean(centered * centered, **LAST_DIM) + LN_EPS)
    return centered * inv_std, inv_std


def fixed(*shape):
    return pl.BlockSpec(shape, lambda *_: (0,) * len(shape))


def by_column(*shape):
    return pl.BlockSpec(shape, lambda j, *_: (0, j))


def aligned(start, size):
    return pl.ds(pl.multiple_of(start, size), size)


def run_all(copies, wait=False):
    for c in copies:
        c.wait() if wait else c.start()


dma = pltpu.SemaphoreType.DMA


def flip(index, bit):
    return index + bit * (1 - 2 * ((index // bit) % 2))


def att_head(q_ref, k_ref, v_ref, do_ref, o_ref, dq_ref, dk_ref, dv_ref, dk_acc, dv_acc):
    to_exp2 = SCALE * math.log2(math.e)
    k_t = k_ref[...]
    v_t = v_ref[...]
    k_n = k_t.T
    v_n = v_t.T
    db_q = jnp.zeros((DH, 1), F32)
    for i in reversed(range(S // BQ)):
        keys = (i + 1) * BQ
        cols = slice(i * BQ, keys)
        q = q_ref[:, cols]
        do = do_ref[:, cols]
        s = dot_nn(k_n[:keys], q)
        row = lax.broadcasted_iota(jnp.int32, (BQ, BQ), 0)
        col = lax.broadcasted_iota(jnp.int32, (BQ, BQ), 1)
        s_diag = jnp.where(row <= col, s[keys - BQ:], -1e30)
        s = jnp.concatenate([s[:keys - BQ], s_diag], axis=0) if i else s_diag
        m = jnp.max(s, **ROWS)
        p = jnp.exp2((s - m) * to_exp2)
        p = p * (1.0 / jnp.sum(p, **ROWS))
        p_low = p.astype(BF16)
        o = dot_nn(v_t[:, :keys], p_low)
        o_ref[:, cols] = o.astype(BF16)
        dp = dot_nn(v_n[:keys], do).astype(BF16).astype(F32)
        row_dot = jnp.sum(o * do.astype(F32), **ROWS)
        ds = (p * (dp - row_dot)).astype(BF16)
        dq = (dot_nn(k_t[:, :keys], ds) * SCALE).astype(BF16)
        dq_ref[:, cols] = dq
        db_q += jnp.sum(dq.astype(F32), **LAST_DIM)
        dk = dot_nt(q, ds)
        dv = dot_nt(do, p_low)
        if keys == S:
            dk_acc[...] = dk
            dv_acc[...] = dv
        else:
            dk_acc[:, :keys] += dk
            dv_acc[:, :keys] += dv
    dk = (dk_acc[...] * SCALE).astype(BF16)
    dv = dv_acc[...].astype(BF16)
    dk_ref[...] = dk
    dv_ref[...] = dv
    return db_q, jnp.sum(dk.astype(F32), **LAST_DIM), jnp.sum(dv.astype(F32), **LAST_DIM)


NEAR = (2, 4, 8)
VIA = {6: 4, 12: 8, 10: 2}
LAST = {12: 2, 10: 4, 6: 8}
SLOT = {d: i for i, d in enumerate((0, 2, 4, 8, 6, 12, 10, 14))}
N_SEND, N_RECV = 17, 9
GY, U = 1, 0
FAR = list(SLOT)[1:]
ATT = [(0, 0)] * GH
STEPS = [(b, 0) for b in range(B)] + [(0, d) for d in FAR] + ATT + [(1, d) for d in FAR] + ATT
AT0 = B + len(FAR)
AT1 = len(STEPS) - GH
NEXT1 = AT0 + GH
FETCH_HERE = (0, 2, 5, 8, NEXT1, 16, 17)
FETCH_NEXT = (0, 2, 3, 5, 6, NEXT1, 14, 17, 18)


def front_kernel(*refs):
    x_ref, gy_ref, gain_ref, lnb_ref, w_ref, wout_ref, bias_ref = refs[:7]
    all_ref, *piece_refs = refs[7:12]
    far_refs = refs[12:15]
    db_ref = refs[15]
    (wt_ref, wo_ref, qkv_ref, do_ref, pair_ref, head_ref, u_ref, dk_acc, dv_acc,
     send_sem, recv_sem, peer_sem, own_sem, pair_sem, head_sem, w_sem, osend_sem, orecv_sem) = refs[16:]
    me = lax.axis_index("sp")
    near = {bit: flip(me, bit) for bit in NEAR}
    peer = flip(me, 1)
    src = {0: me, **near}
    src[6], src[12], src[10] = flip(near[2], 4), flip(near[4], 8), flip(near[8], 2)
    src[14] = flip(src[6], 8)
    chip = me // 2
    group = chip + (chip // 4) * (7 - 2 * chip)
    mine = 4 * (me % 2) + group
    third = D // 3
    mesh_id = pl.DeviceIdType.MESH
    sends = []

    def half(b, d, h):
        return all_ref.at[b, d, pl.ds(h * TOK, TOK)]

    def descriptor(b, h, n, kind, d):
        source = target = half(b, src[d if kind else 0], h)
        if kind == 0:
            source = own_rows(b, h)
            recv, to = recv_sem.at[b, h, SLOT[d] - 1], near[d]
        elif kind == 1:
            far = [e for e in VIA if VIA[e] == d][0]
            recv, to = recv_sem.at[b, h, SLOT[far] - 1], near[far - d]
        elif kind == 2:
            j = list(LAST).index(d)
            source = target = source.at[:, pl.ds(j * third, third)]
            recv, to = recv_sem.at[b, h, 6 + j], near[LAST[d]]
        else:
            if d == 0:
                source = own_rows(b, h)
            recv, to = peer_sem.at[b, h, SLOT[d]], peer
        return pltpu.make_async_remote_copy(
            src_ref=source, dst_ref=target, send_sem=send_sem.at[b, h, n], recv_sem=recv,
            device_id=(to,), device_id_type=mesh_id)

    def send(b, h, kind, d):
        spec = (b, h, sum(1 for other in sends if other[:2] == (b, h)), kind, d)
        sends.append(spec)
        descriptor(*spec).start()

    def arrived(target, sem):
        pltpu.make_async_copy(target, target, sem).wait()

    def own_rows(b, h):
        return gy_ref.at[b] if h == GY else half(b, me, U)

    def stage0(b, h):
        for bit in NEAR:
            send(b, h, 0, bit)

    def stage0_peer(b, h):
        send(b, h, 3, 0)

    def stage1(b, h):
        for d in NEAR:
            arrived(half(b, src[d], h), recv_sem.at[b, h, SLOT[d] - 1])
            send(b, h, 1, d)
            send(b, h, 3, d)

    def stage2(b, h):
        for d in LAST:
            arrived(half(b, src[d], h), recv_sem.at[b, h, SLOT[d] - 1])
            send(b, h, 2, d)
            send(b, h, 3, d)

    def stage3(b, h):
        for j in range(3):
            arrived(half(b, src[14], h).at[:, pl.ds(j * third, third)], recv_sem.at[b, h, 6 + j])
        send(b, h, 3, 14)

    def look_up(k, values):
        return sum(jnp.where(k == i, v, 0) for i, v in enumerate(values) if v)

    def pair_of(k):
        flips = look_up(k, [d // 2 for _, d in STEPS])
        x, y, z = (chip % 2 + flips) % 2, (chip // 2 + flips // 2) % 2, (chip // 4 + flips // 4) % 2
        return look_up(k, [b for b, _ in STEPS]), x + 2 * y + 4 * z, look_up(k, [SLOT[d] for _, d in STEPS])

    def fetch(k):
        b, source, slot = pair_of(k)
        for h in range(2):
            arrived(half(b, 2 * source, h), peer_sem.at[b, h, slot])
        pair_copy(k).start()

    def pair_copy(k):
        b, source, _ = pair_of(k)
        return pltpu.make_async_copy(all_ref.at[b, pl.ds(2 * source, 2)], pair_ref.at[k % 2], pair_sem.at[k % 2])

    def among(k, steps):
        return sum(jnp.where(k == i, 1, 0) for i in steps) > 0

    def project(k):
        @pl.when(among(k, FETCH_HERE))
        def _():
            fetch(k)

        pair_copy(k).wait()

        @pl.when(among(k, FETCH_NEXT))
        def _():
            fetch(k + 1)

        b, source, _ = pair_of(k)
        pair = pair_ref.at[k % 2]
        u = jnp.concatenate([pair[0, :TOK], pair[1, :TOK]], axis=0)
        gy = jnp.concatenate([pair[0, TOK:], pair[1, TOK:]], axis=0)
        cols = aligned(source * 2 * TOK, 2 * TOK)
        qkv_ref[b, :, cols] = (dot_nt(wt_ref[...], u) + bias_ref[...]).astype(BF16)
        do_ref[b, :, cols] = dot_nt(wo_ref[...], gy).astype(BF16)

    weights = [pltpu.make_async_copy(w_ref.at[t, mine], wt_ref.at[pl.ds(t * GR, GR)], w_sem.at[t]) for t in range(3)]
    weights.append(pltpu.make_async_copy(wout_ref.at[mine], wo_ref, w_sem.at[3]))
    for c in weights:
        c.start()

    barrier = pltpu.get_barrier_semaphore()
    for d in (peer, *near.values()):
        pl.semaphore_signal(barrier, inc=1, device_id=(d,), device_id_type=mesh_id)
    pl.semaphore_wait(barrier, 4)

    stage0(0, GY)
    for b in range(B):
        load = pltpu.make_async_copy(gy_ref.at[b], pair_ref.at[b, 0, pl.ds(TOK, TOK)], own_sem.at[3 * b])
        load.start()
        x = x_ref[b].astype(F32)
        u_ref[b] = (normalize(x)[0] * gain_ref[...] + lnb_ref[...]).astype(BF16)
        store = [pltpu.make_async_copy(u_ref.at[b], half(b, me, U), own_sem.at[3 * b + 1])]
        store[0].start()
        load.wait()
        store.append(pltpu.make_async_copy(pair_ref.at[b, 0, pl.ds(TOK, TOK)], half(b, me, GY), own_sem.at[3 * b + 2]))
        store[1].start()
        for c in store:
            c.wait()
        if b == 0:
            stage0(0, U)
        stage0_peer(b, U)
        stage0_peer(b, GY)
    for c in weights:
        c.wait()

    def head_of(ref, i):
        return ref.at[aligned((i % GH) * DH, DH), aligned((i // GH) * S, S)]

    def local_copies(i):
        return [pltpu.make_async_copy(head_ref.at[i % 2, n], head_of(ref, i), head_sem.at[i % 2, n])
                for n, ref in enumerate(piece_refs)]

    def o_copies(i):
        return [pltpu.make_async_remote_copy(
            src_ref=head_of(piece_refs[0], i), dst_ref=head_of(far_refs[n], i), send_sem=osend_sem.at[i, n],
            recv_sem=orecv_sem.at[i, n], device_id=(near[bit],), device_id_type=mesh_id)
            for n, bit in enumerate(NEAR)]

    def stored(i):
        for c in local_copies(i):
            c.wait()

    def pass_on(i):
        for c in o_copies(i):
            c.start()

    def attend(i):
        b, h = i // GH, i % GH
        rows = lambda ref, t: ref.at[b, aligned(t * GR + h * DH, DH)]
        out = [head_ref.at[i % 2, n] for n in range(len(piece_refs))]
        sums = att_head(*(rows(qkv_ref, t) for t in range(3)), rows(do_ref, 0), *out, dk_acc, dv_acc)
        for t, db in enumerate(sums):
            db_ref[b, t, aligned(h * DH, DH), :] = jnp.broadcast_to(db, (DH, LANES))
        for c in local_copies(i):
            c.start()

        @pl.when(h > 0)
        def _():
            stored(i - 1)

        @pl.when(i > GH)
        def _():
            pass_on(i - 1)

    def first_o():
        stored(GH - 1)
        for i in range(GH):
            pass_on(i)

    duties = {
        2: [lambda: stage1(0, GY), lambda: stage1(0, U)],
        5: [lambda: stage2(0, GY), lambda: stage2(0, U), lambda: stage0(1, GY), lambda: stage0(1, U)],
        8: [lambda: stage3(0, GY), lambda: stage3(0, U)],
        AT0 + 1: [lambda: stage1(1, GY)],
        AT0 + 2: [lambda: stage1(1, U)],
        NEXT1: [lambda: stage2(1, GY)],
        15: [lambda: stage2(1, U)],
        17: [lambda: stage3(1, GY), lambda: stage3(1, U), first_o],
    }

    def step(k, carry):
        for at, calls in duties.items():
            @pl.when(k == at)
            def _():
                for call in calls:
                    call()

        attending = jnp.logical_or(jnp.logical_and(k >= AT0, k < NEXT1), k >= AT1)

        @pl.when(attending)
        def _():
            attend(k - jnp.where(k < NEXT1, AT0, AT1 - GH))

        @pl.when(jnp.logical_not(attending))
        def _():
            project(k)

        return carry

    lax.fori_loop(0, len(STEPS), step, 0)
    stored(B * GH - 1)
    pass_on(B * GH - 1)
    for spec in sends:
        descriptor(*spec).wait_send()
    for i in range(B * GH):
        for c in o_copies(i):
            c.wait()


def front(x_in, grad_y, gain, ln_bias, w_rows, w_out, bias):
    vmem = pl.BlockSpec(memory_space=pltpu.VMEM)
    anywhere = pl.BlockSpec(memory_space=pl.ANY)
    gathered = jax.ShapeDtypeStruct((B, NDEV, 2 * TOK, D), BF16)
    piece = jax.ShapeDtypeStruct((GR, B * S), BF16)
    return pl.pallas_call(
        front_kernel,
        in_specs=[vmem, anywhere, vmem, vmem, anywhere, anywhere, vmem],
        out_specs=[anywhere] * 8 + [vmem],
        out_shape=[gathered] + [piece] * 7 + [jax.ShapeDtypeStruct((B, 3, GR, LANES), F32)],
        scratch_shapes=[
            pltpu.VMEM((3 * GR, D), BF16),
            pltpu.VMEM((GR, D), BF16),
            pltpu.VMEM((B, 3 * GR, S), BF16),
            pltpu.VMEM((B, GR, S), BF16),
            pltpu.VMEM((2, 2, 2 * TOK, D), BF16),
            pltpu.VMEM((2, 4, DH, S), BF16),
            pltpu.VMEM((B, TOK, D), BF16),
            pltpu.VMEM((DH, S), F32),
            pltpu.VMEM((DH, S), F32),
            dma((B, 2, N_SEND)),
            dma((B, 2, N_RECV)),
            dma((B, 2, 8)),
            dma((6,)),
            dma((2,)),
            dma((2, 4)),
            dma((4,)),
            dma((B * GH, 3)),
            dma((B * GH, 3)),
        ],
        compiler_params=params(collective_id=0, has_side_effects=True),
        cost_estimate=cost(15e10, 2e8),
        name="front",
    )(x_in, grad_y, gain.reshape(1, D), ln_bias.reshape(1, D), w_rows, w_out.reshape(8, GR, D), bias)


def my_group(tbl, s):
    return aligned(tbl[3 + s] * GR, GR)


def collect_kernel(tbl, *refs):
    for s in range(4):
        for k in range(4):
            refs[-1][k * TOK:(k + 1) * TOK, my_group(tbl, s)] = refs[4 * k + s][...].T


def collect(tbl, pieces):
    spec = lambda k: pl.BlockSpec((GR, TOK), lambda i, t: (0, (k % B) * NDEV + t[1 + k // B]))
    return pl.pallas_call(
        collect_kernel,
        grid_spec=pltpu.PrefetchScalarGridSpec(
            num_scalar_prefetch=1, grid=(1,), in_specs=[spec(k) for k in range(4) for _ in pieces],
            out_specs=fixed(2 * B * TOK, CR)),
        out_shape=jax.ShapeDtypeStruct((2 * B * TOK, CR), BF16),
        compiler_params=params(),
        cost_estimate=cost(1e9, 3e6),
        name="collect",
    )(tbl, *pieces * 4)


BD = 256
SPLIT = 3


def dw_kernel(t, groups, n_in, rows_at, puts, times, tbl, x0, x1, *refs):
    pieces = refs[:4]
    outs = refs[n_in:]
    buf_ref, ex_ref = outs[:2]
    lhs_ref, own_ref, sem, own_sem, ex_sem, put_sem = outs[-6:]
    j = pl.program_id(0)
    core = tbl[0]
    extra = list(refs[4:n_in])

    @pl.when(j == 0)
    def _():
        for wait in (False, True):
            for s, piece in enumerate(pieces):
                place = tbl[3 + s] - groups[0]

                @pl.when(jnp.logical_and(place >= 0, tbl[3 + s] < groups[1]))
                def _():
                    run_all([pltpu.make_async_copy(piece, lhs_ref.at[aligned(place * GR, GR)], sem.at[s])], wait)

    def columns(step):
        return aligned(step * BD, BD)

    def own_out(step):
        src = own_ref.at[step % 2]
        start = (2 * t + core) * CR + groups[0] * GR
        rows = pl.ds(pl.multiple_of(start, GR), own_ref.shape[1])
        return (pltpu.make_async_copy(src, buf_ref.at[rows, columns(step)], own_sem.at[step % 2]),
                pltpu.make_async_copy(src, ex_ref.at[:, columns(step)], ex_sem.at[step % 2]))

    put_copies = []
    for n, (at, row_block) in enumerate(puts):
        rows = aligned((2 * row_block + 1 - core) * CR, CR)
        put_copies.append(pltpu.make_async_copy(extra.pop(0), outs[at].at[rows, columns(j)], put_sem.at[n]))
    run_all(put_copies)

    x = jnp.concatenate([ref[0, r] for ref in (x0, x1) for r in range(NDEV)], axis=0)
    res = dot_nn(lhs_ref[...], x)
    if times is not None:
        part = dot_nn(extra[0][...], extra[1][...])
        for k in range(2):
            outs[times + k][...] = part[k * B * TOK:(k + 1) * B * TOK]

    @pl.when(j >= 2)
    def _():
        run_all(own_out(j - 2), True)

    own_ref[j % 2] = res
    run_all(own_out(j))

    if rows_at is not None:
        @pl.when(j == 0)
        def _():
            for k in range(4):
                cols = aligned((k % B) * S + tbl[1 + k // B] * TOK, TOK)
                outs[rows_at][k * TOK:(k + 1) * TOK, :] = lhs_ref[:, cols].T

    run_all(put_copies, True)

    @pl.when(j == pl.num_programs(0) - 1)
    def _():
        run_all(own_out(j - 1) + own_out(j), True)


def weight_grad(tbl, gathered, pieces, t, which, out_rows, prev=None, rows=True, puts=(), times=None, groups=(0, 4)):
    n_rows = (groups[1] - groups[0]) * GR
    anywhere = pl.BlockSpec(memory_space=pl.ANY)
    x_spec = lambda b: pl.BlockSpec((1, NDEV, TOK, BD), lambda j, t: (b, 0, which, j))
    ins = [(x_spec(b), gathered) for b in range(B)] + [(anywhere, p) for p in pieces]
    outs = [(anywhere, (out_rows, D), F32), (anywhere, (n_rows, D), F32)]
    rows_at = times_at = None
    put_at = []
    whole = fixed(2 * B * TOK, CR)
    if rows:
        rows_at = len(outs)
        outs.append((whole, (2 * B * TOK, CR), BF16))
    if times is not None:
        times_at = len(outs)
        outs += [(by_column(B * TOK, BD), (B * TOK, D), F32)] * 2
    ins += [(by_column(CR, BD), block) for block, *_ in puts]
    if times is not None:
        ins.append((whole, times[0]))
        ins.append((pl.BlockSpec((CR, BD), lambda j, t: (2 * times[2] + t[0], j)), times[1]))
    alias = {}
    if prev is not None:
        alias[1 + len(ins)] = 0
        ins.append((anywhere, prev))
    for _, row_block, buffer in puts:
        put_at.append((0 if buffer is None else len(outs), row_block))
        if buffer is not None:
            alias[1 + len(ins)] = len(outs)
            ins.append((anywhere, buffer))
            outs.append((anywhere, buffer.shape, F32))
    return pl.pallas_call(
        functools.partial(dw_kernel, t, groups, len(ins) - B, rows_at, put_at, times_at),
        grid_spec=pltpu.PrefetchScalarGridSpec(
            num_scalar_prefetch=1,
            grid=(D // BD,),
            in_specs=[spec for spec, _ in ins],
            out_specs=[spec for spec, *_ in outs],
            scratch_shapes=[
                pltpu.VMEM((n_rows, B * S), BF16),
                pltpu.VMEM((2, n_rows, BD), F32),
                dma((4,)), dma((2,)), dma((2,)), dma((2,)),
            ]),
        out_shape=[jax.ShapeDtypeStruct(*shape) for _, *shape in outs],
        input_output_aliases=alias,
        compiler_params=params(),
        cost_estimate=cost(2 * n_rows * D * B * S, 75e6),
        name="weight_grad",
    )(tbl, *(arg for _, arg in ins))


CB = 512


def contract_kernel(n, *refs):
    rows = jnp.concatenate([r[...] for r in refs[1:1 + n]], axis=1)
    weight = jnp.concatenate([r[...] for r in refs[1 + n:1 + 2 * n]], axis=0)
    acc = dot_nn(rows, weight)
    for k, prev in enumerate(refs[1 + 2 * n:-2]):
        refs[k - 2][...] = acc[k * B * TOK:(k + 1) * B * TOK] + prev[...]


def contract(tbl, rows, weight, blocks, prev):
    out = by_column(B * TOK, CB)
    w_spec = lambda block: pl.BlockSpec((CR, CB), lambda i, t: (2 * block + t[0], i))
    n = len(blocks)
    return pl.pallas_call(
        functools.partial(contract_kernel, n),
        grid_spec=pltpu.PrefetchScalarGridSpec(
            num_scalar_prefetch=1,
            grid=(D // CB,),
            in_specs=[fixed(2 * B * TOK, CR)] * n
            + [w_spec(block) for block in blocks] + [out] * 2,
            out_specs=[out] * 2),
        out_shape=[jax.ShapeDtypeStruct((B * TOK, D), F32)] * 2,
        compiler_params=params(),
        cost_estimate=cost(2 * B * TOK * D * D * n, 22e6),
        name="contract",
    )(tbl, *rows, *[weight] * n, *prev)


def finish_kernel(du_own, du_peer, x_ref, gy_ref, db_ref, gain_ref, gx_ref, sums_ref):
    x_hat, inv_std = normalize(x_ref[0].astype(F32))
    du = (du_own[...] + du_peer[...]).astype(BF16).astype(F32)
    gy = gy_ref[0].astype(F32)
    grad_hat = du * gain_ref[...]
    centered = grad_hat - jnp.mean(grad_hat, **LAST_DIM)
    gx_ref[0] = (gy + inv_std * (centered - x_hat * jnp.mean(grad_hat * x_hat, **LAST_DIM))).astype(BF16)

    @pl.when(pl.program_id(0) == 0)
    def _():
        sums_ref[...] = db_ref[...]

    for k, val in enumerate((du * x_hat, du, gy)):
        sums_ref[k:k + 1, :] += jnp.sum(val, **ROWS)


def finish_y_kernel(y_own, y_peer, x_ref, b_ref, y_ref):
    y_ref[0] = (x_ref[0].astype(F32) + (y_own[...] + y_peer[...] + b_ref[...])).astype(BF16)


def finish(kernel, partials, acts, vector, sums=None):
    more = [] if sums is None else [sums]
    act = pl.BlockSpec((1, TOK, D), lambda b: (b, 0, 0))
    grad = jax.ShapeDtypeStruct((B, TOK, D), BF16)
    return pl.pallas_call(
        kernel,
        grid=(B,),
        in_specs=[pl.BlockSpec((TOK, D), lambda b: (b, 0))] * len(partials) + [act] * len(acts)
        + [fixed(8, D) for _ in more] + [fixed(1, D)],
        out_specs=[act] + [fixed(8, D) for _ in more],
        out_shape=[grad] + [jax.ShapeDtypeStruct((8, D), F32) for _ in more],
        compiler_params=params(),
        cost_estimate=cost(1e8, 1e7),
        name="finish",
    )(*partials, *acts, *more, vector.reshape(1, D))


def solution(mesh):
    def permute(a, bit):
        return lax.ppermute(a, "sp", [(i, i ^ bit) for i in range(NDEV)])

    def block(x_in, grad_y, ln_gain, ln_bias, w_qkv, b_qkv, w_out, b_out):
        me = lax.axis_index("sp")
        core, chip = me % 2, me // 2
        group = lambda c: jnp.where(c < 4, c, 7 - c)
        groups = [group(chip ^ d) for d in (0, 1, 2, 4)]
        tbl = jnp.stack([core, me, me ^ 1] + groups).astype(jnp.int32)
        mine = 4 * core + groups[0]

        flat_w = jnp.transpose(w_qkv, (1, 2, 3, 0)).reshape(3 * D, D)
        bias = lax.dynamic_slice_in_dim(b_qkv.reshape(3, 8, GR), mine, 1, axis=1).reshape(3 * GR, 1)
        gathered, o, dq, dk, dv, *far_o, db = front(
            x_in, grad_y, ln_gain, ln_bias, flat_w.reshape(3, 8, GR, D), w_out, bias)

        pieces = {"o": [o] + far_o}
        for name, piece in (("v", dv), ("k", dk), ("q", dq)):
            pieces[name] = [piece] + [permute(piece, bit) for bit in NEAR]

        def swap(a):
            return permute(a, 1)

        def grad(name, *args, **kw):
            return weight_grad(tbl, gathered, pieces[name[0]], *args, **kw)

        gwo, ex_o, rows_o = grad("o", 0, GY, D)
        ex_o = swap(ex_o)
        gwq, ex_v, rows_v, y_own, y_peer = grad("v", 2, U, 3 * D, times=(rows_o, w_out.reshape(D, D), 0))
        y_peer = swap(y_peer)
        ex_v = swap(ex_v)
        gwq, ex_k, rows_k, *du, gwo = grad("k", 1, U, 3 * D, gwq, puts=[(ex_o, 0, gwo)], times=(rows_v, flat_w, 2))
        rows_q = collect(tbl, pieces["q"])
        ex_k = swap(ex_k)
        du_own, du_peer = contract(tbl, [rows_k, rows_q], flat_w, [1, 0], du)
        du_peer = swap(du_peer)
        y_out, = finish(finish_y_kernel, [y_own, y_peer], [x_in], b_out)
        db = jnp.where(chip < 4, db[0, :, :, 0] + db[1, :, :, 0], 0.0).reshape(3, 1, GR)
        sums = lax.dynamic_update_slice(jnp.zeros((8, 8, GR), F32), db, (3, mine, 0)).reshape(8, D)
        grad_x, sums = finish(finish_kernel, [du_own, du_peer], [x_in, grad_y], ln_gain, sums)
        parts = [(0, SPLIT), (SPLIT, 4)]
        gwq, ex_q0 = grad("q0", 0, U, 3 * D, gwq, rows=False, puts=[(ex_v, 2, None), (ex_k, 1, None)], groups=parts[0])
        ex_q0 = swap(ex_q0)
        gwq, ex_q1 = grad("q1", 0, U, 3 * D, gwq, rows=False, groups=parts[1])
        ex_q1 = swap(ex_q1)
        for bit in (1, *NEAR):
            sums = sums + permute(sums, bit)
        for ex, part in ((ex_q0, parts[0]), (ex_q1, parts[1])):
            gwq = lax.dynamic_update_slice(gwq, ex, ((1 - core) * CR + part[0] * GR, 0))

        grad_w_qkv = jnp.transpose(gwq.reshape(3, NH, DH, D), (3, 0, 1, 2))
        grad_b_qkv = sums[3:6].reshape(3, NH, DH)
        return y_out, grad_x, sums[0], sums[1], grad_w_qkv, grad_b_qkv, gwo.reshape(NH, DH, D), sums[2]

    seq, rep = P(None, "sp", None), P()
    specs = (seq, seq) + (rep,) * 6
    return jax.shard_map(block, mesh=mesh, in_specs=specs, out_specs=specs, check_vma=False)
```

time: 2050 us -> 725 us (0.35)
  waiting for transfers between devices: 1160 us -> 153 us
  Pallas kernels: 0 us -> 529 us
  matrix products: 414 us -> 0 us
  local copies, waits for them, and re-layouts: 277 us -> 23.4 us
  blocking collectives: 130 us -> 0 us
  other arithmetic: 29.7 us -> 4.03 us
    psum x3 -> x0, waiting for transfers between devices: 1110 us -> none  [local_block(): lax.psum((grad_ln_gain, grad_ln_bias, grad_w_qkv, grad_b_qkv, grad_w_out,...]
    pallas_call x0 -> x10, Pallas kernels: none -> 529 us  [the longest x5 258 us: weight_grad(): pl.pallas_call(functools.partial(dw_kernel, t, groups, len(ins) - B, rows...]
    dot_general x16 -> x0, matrix products: 336 us -> none  [the longest x2 67 us: head_attention_bwd(): jnp.einsum('crl,crf->clf', grad_s, qkv_head[0], preferred_element_type=jn...]
    ppermute x0 -> x20, waiting for transfers between devices: none -> 153 us  [permute(): return lax.ppermute(a, 'sp', [(i, i ^ bit) for i in range(NDEV)])]
    all_to_all x2 -> x0, blocking collectives: 130 us -> none  [the longest x1 76.9 us: local_block(): grad_qkv_local = lax.all_to_all(grad_qkv_heads, 'sp', 3, 0, tiled=True)]
    unnamed x44 -> x0, local copies, waits for them, and re-layouts: 109 us -> none
    sub x4 -> x0, matrix products: 78.2 us -> none  [head_probs(): return jax.nn.softmax(scores, axis=-1)]
    dot_general x1 -> x0, local copies, waits for them, and re-layouts: 74.6 us -> none  [local_block(): jnp.einsum('bsd,htbse->dthe', normed, grad_qkv_local, preferred_element_t...]
  transfers between devices with their start and end apart: 5 -> 20, of which waited for: 3 -> 10; matrix products, arithmetic and copies ran while one was open for 14% -> 3% of each run, Pallas kernels for 0% -> 25%
where the time goes in v2:
time: 725 us; the launch traced here: 724 us
  Pallas kernels  529 us (73%)
  waiting for transfers between devices  153 us (21%)
  local copies, waits for them, and re-layouts  23.4 us (3%)
  starting transfers between devices  14.2 us (2%)
    pallas_call x5, Pallas kernels, weight_grad(): pl.pallas_call(functools.partial(dw_kernel, t, groups, len(ins) - B, rows...  258 us
    pallas_call x1, Pallas kernels, front(): pl.pallas_call(front_kernel, in_specs=[vmem, anywhere, vmem, vmem, anywhe...  237 us
    ppermute x20, waiting for transfers between devices, permute(): return lax.ppermute(a, 'sp', [(i, i ^ bit) for i in range(NDEV)])  153 us
    pallas_call x1, Pallas kernels, contract(): pl.pallas_call(functools.partial(contract_kernel, n), grid_spec=pltpu.Pre...  17.8 us
    dynamic_update_slice x2, local copies, waits for them, and re-layouts, block(): gwq = lax.dynamic_update_slice(gwq, ex, ((1 - core) * CR + part[0] * GR, 0))  17.4 us
  transfers between devices with their start and end apart: 20, of which 10 were waited for; matrix products, arithmetic and copies ran while one was open for 3% of the time, Pallas kernels for 25%

profile of v2, /device:TPU:0, one launch (start us, length us, event | category | flops | bytes accessed | tf_op | source)
XLA Modules:
  0.0 724.3 jit_solution(8801356882853434887)
XLA Ops:
  0.7 0.9 reshape.81
  1.6 1.1 copy.25.refs_6_
  2.6 0.7 stack.31.tbl.refs_0_
  3.3 236.9 %front.1 = (bf16[2,16,256,3072]{3,2,1,0:T(8,128)(2,1)}, bf16[384,4096]{1,0:T(8,128)(2,1)}, bf16[384,4096]{1,0:T(8,128)(2,1)}, bf16[384,4096]{1,0:T(8,128)(2,1)},...) custom-call(bf16[2,128,3072]{2,1,0:T(8,128)(2,1)} %x_ref.3, ...), custom_call_target="tpu_custom_call" | custom-call | flops 149999992832 | bytes 200000000 | tf_op jit(solution)/shard_map/front/pallas_call | solution.py:375
  240.3 54.2 %weight_grad.5 = (f32[3072,3072]{1,0:T(8,128)}, f32[1536,3072]{1,0:T(8,128)}, bf16[512,1536]{1,0:T(8,128)(2,1)}) custom-call(s32[7]{0:T(128)} %stack.31.tbl.refs_0_, bf16[2,16,256,3072]{3,2,1,0:T(8,128)(2,1)} %get-tuple-element.39.x0.x1, bf16[2,16,256,3072]{3,2,1,0:T(8,128)(2,1)} %get-tuple-element.39.x0.x1, bf16[384,4096]{1,0:T(8,128)(2,1)} %get-tuple-element.41.refs_0_, ...), custom_call_target="tpu_custom_call" | custom-call | flops 38654705664 | bytes 75000000 | tf_op jit(solution)/shard_map/weight_grad/pallas_call | solution.py:526
  294.5 0.9 collective-permute-start
  295.4 1.2 collective-permute-start.1
  296.5 0.9 collective-permute-start.2
  297.4 1.1 collective-permute-start.4
  298.5 67.3 %collective-permute-done.refs_1_ = bf16[384,4096]{1,0:T(8,128)(2,1)} collective-permute-done((bf16[384,4096]{1,0:T(8,128)(2,1)}, bf16[384,4096]{1,0:T(8,128)(2,1)}, u32[]{:S(2)}, u32[]{:S(2)}) %collective-permute-start) | collective-permute-done | bytes 3145760 | tf_op jit(solution)/shard_map/ppermute | solution.py:615
  365.8 0.8 collective-permute-start.5
  366.6 1.2 collective-permute-start.6
  367.8 60.1 %weight_grad.6 = (f32[9216,3072]{1,0:T(8,128)}, f32[1536,3072]{1,0:T(8,128)}, bf16[512,1536]{1,0:T(8,128)(2,1)}, f32[256,3072]{1,0:T(8,128)}, f32[256,3072]{1,0:T(8,128)}) custom-call(s32[7]{0:T(128)} %stack.31.tbl.refs_0_, bf16[2,16,256,3072]{3,2,1,0:T(8,128)(2,1)} %get-tuple-element.39.x0.x1, bf16[2,16,256,3072]{3,2,1,0:T(8,128)(2,1)} %get-tuple-element.39.x0.x1, ...), custom_call_target="tpu_custom_call" | custom-call | flops 38654705664 | bytes 75000000 | tf_op jit(solution)/shard_map/weight_grad/pallas_call | solution.py:526
  427.9 4.8 collective-permute-done.4.refs_1_
  432.7 2.5 collective-permute-done.5.refs_2_
  435.2 0.5 collective-permute-done.6.refs_3_
  435.8 67.4 %weight_grad.7 = (f32[9216,3072]{1,0:T(8,128)}, f32[1536,3072]{1,0:T(8,128)}, bf16[512,1536]{1,0:T(8,128)(2,1)}, f32[256,3072]{1,0:T(8,128)}, f32[256,3072]{1,0:T(8,128)}, /*index=5*/f32[3072,3072]{1,0:T(8,128)}) custom-call(s32[7]{0:T(128)} %stack.31.tbl.refs_0_, ...), custom_call_target="tpu_custom_call", output_to_operand_aliasing={{0}: (10, {}), {5}: (11, {})} | custom-call | flops 38654705664 | bytes 75000000 | tf_op jit(solution)/shard_map/weight_grad/pallas_call | solution.py:526
  503.3 1.2 collective-permute-start.8
  504.5 0.9 collective-permute-start.9
  505.4 1.2 collective-permute-start.10
  506.5 67.5 %collective-permute-done.8.refs_1_.refs_5_.refs_9_.refs_13_ = bf16[384,4096]{1,0:T(8,128)(2,1)} collective-permute-done((bf16[384,4096]{1,0:T(8,128)(2,1)}, bf16[384,4096]{1,0:T(8,128)(2,1)}, u32[]{:S(2)}, u32[]{:S(2)}) %collective-permute-start.8) | collective-permute-done | bytes 3145760 | tf_op jit(solution)/shard_map/ppermute | solution.py:615
  574.1 0.9 collective-permute-done.9.refs_2_.refs_6_.refs_10_.refs_14_
  575.0 0.6 collective-permute-done.10.refs_3_.refs_7_.refs_11_.refs_15_
  575.6 54.2 %weight_grad.8 = (f32[9216,3072]{1,0:T(8,128)}, f32[1152,3072]{1,0:T(8,128)}) custom-call(s32[7]{0:T(128)} %stack.31.tbl.refs_0_, bf16[2,16,256,3072]{3,2,1,0:T(8,128)(2,1)} %get-tuple-element.39.x0.x1, bf16[2,16,256,3072]{3,2,1,0:T(8,128)(2,1)} %get-tuple-element.39.x0.x1, ...), custom_call_target="tpu_custom_call", output_to_operand_aliasing={{0}: (9, {})} | custom-call | flops 28991029248 | bytes 75000000 | tf_op jit(solution)/shard_map/weight_grad/pallas_call | solution.py:526
  629.8 0.5 collective-permute-start.3
  630.3 3.8 collect.1.refs_2_
  634.1 17.8 %contract.1 = (f32[256,3072]{1,0:T(8,128)}, f32[256,3072]{1,0:T(8,128)}) custom-call(s32[7]{0:T(128)} %stack.31.tbl.refs_0_, bf16[512,1536]{1,0:T(8,128)(2,1)} %get-tuple-element.53.refs_1_, bf16[512,1536]{1,0:T(8,128)(2,1)} %collect.1.refs_2_, bf16[9216,3072]{1,0:T(8,128)(2,1)} %bitcast.29, bf16[9216,3072]{1,0:T(8,128)(2,1)} %bitcast.30, ...), custom_call_target="tpu_custom_call" | custom-call | flops 9663676416 | bytes 22000000 | tf_op jit(solution)/shard_map/contract/pallas_call | solution.py:561
  652.0 22.6 %weight_grad.9 = (f32[9216,3072]{1,0:T(8,128)}, f32[384,3072]{1,0:T(8,128)}) custom-call(s32[7]{0:T(128)} %stack.31.tbl.refs_0_, bf16[2,16,256,3072]{3,2,1,0:T(8,128)(2,1)} %get-tuple-element.39.x0.x1, bf16[2,16,256,3072]{3,2,1,0:T(8,128)(2,1)} %get-tuple-element.39.x0.x1, ...), custom_call_target="tpu_custom_call", output_to_operand_aliasing={{0}: (7, {})} | custom-call | flops 9663676416 | bytes 75000000 | tf_op jit(solution)/shard_map/weight_grad/pallas_call | solution.py:526
  674.5 0.5 collective-permute-start.19
  675.0 1.5 select_reduce_fusion
  676.5 0.6 broadcast_in_dim.7
  677.2 1.3 dynamic_update_slice.9
  678.5 7.8 %finish.3 = (bf16[2,128,3072]{2,1,0:T(8,128)(2,1)}, f32[8,3072]{1,0:T(8,128)}) custom-call(f32[256,3072]{1,0:T(8,128)} %get-tuple-element.57.du_own, f32[256,3072]{1,0:T(8,128)} %collective-permute-done.11.du_peer, bf16[2,128,3072]{2,1,0:T(8,128)(2,1)} %x_ref.3, bf16[2,128,3072]{2,1,0:T(8,128)(2,1)} %gy_ref.1, f32[8,3072]{1,0:T(8,128)} %bitcast.15.db_ref, ...), custom_call_target="tpu_custom_call" | custom-call | flops 100000000 | bytes 10000000 | tf_op jit(solution)/shard_map/finish/pallas_call | solution.py:600
  686.4 0.1 collective-permute-start.12
  686.4 1.5 collective-permute-done.12
  687.9 0.9 add.50
  688.8 1.2 collective-permute-start.13
  690.0 3.7 collective-permute-done.13
  693.7 1.2 collective-permute-start.14
  694.9 3.4 collective-permute-done.14
  698.3 0.7 add.52
  699.0 1.2 collective-permute-start.15
  700.2 4.4 finish.2
  704.5 1.0 add.53
  705.5 0.7 reshape.88
  706.2 0.6 fusion
  706.9 12.4 %constant_dynamic-update-slice_fusion.1 = f32[9216,3072]{1,0:T(8,128)} fusion(f32[9216,3072]{1,0:T(8,128)} %get-tuple-element.66, f32[1152,3072]{1,0:T(8,128)} %collective-permute-done.18, s32[]{:T(128)S(6)} %select_n.61), kind=kLoop, calls=%fused_computation.2 | loop fusion | bytes 28311556 | tf_op jit(solution)/shard_map/dynamic_update_slice | solution.py:662
  719.2 5.1 constant_dynamic-update-slice_fusion
  (18 shorter events, 0.3 us)
Async XLA Ops:
  294.4 141.3 %collective-permute-start.7 = (f32[1536,3072]{1,0:T(8,128)}, f32[1536,3072]{1,0:T(8,128)}, u32[]{:S(2)}, u32[]{:S(2)}) collective-permute-start(f32[1536,3072]{1,0:T(8,128)} %get-tuple-element.49), channel_id=1, source_target_pairs={{0,1},{1,0},{2,3},{3,2},{4,5},{5,4},{6,7},{7,6},{8,9},{9,8},{10,11... | collective-permute-start | bytes 56623112 | tf_op jit(solution)/shard_map/ppermute | solution.py:615
  294.5 71.3 %collective-permute-start = (bf16[384,4096]{1,0:T(8,128)(2,1)}, bf16[384,4096]{1,0:T(8,128)(2,1)}, u32[]{:S(2)}, u32[]{:S(2)}) collective-permute-start(bf16[384,4096]{1,0:T(8,128)(2,1)} %get-tuple-element.40.refs_0_), channel_id=1, source_target_pairs={{0,2},{1,3},{2,0},{3,1},{4,6},{5,7},{6,4},{7,5},{8,10},{9,11},{10,... | collective-permute-start | bytes 9437192 | tf_op jit(solution)/shard_map/ppermute | solution.py:615
  295.4 71.3 %collective-permute-start.1 = (bf16[384,4096]{1,0:T(8,128)(2,1)}, bf16[384,4096]{1,0:T(8,128)(2,1)}, u32[]{:S(2)}, u32[]{:S(2)}) collective-permute-start(bf16[384,4096]{1,0:T(8,128)(2,1)} %get-tuple-element.40.refs_0_), channel_id=1, source_target_pairs={{0,4},{1,5},{2,6},{3,7},{4,0},{5,1},{6,2},{7,3},{8,12},{9,13},{10,... | collective-permute-start | bytes 9437192 | tf_op jit(solution)/shard_map/ppermute | solution.py:615
  296.5 71.3 %collective-permute-start.2 = (bf16[384,4096]{1,0:T(8,128)(2,1)}, bf16[384,4096]{1,0:T(8,128)(2,1)}, u32[]{:S(2)}, u32[]{:S(2)}) collective-permute-start(bf16[384,4096]{1,0:T(8,128)(2,1)} %get-tuple-element.40.refs_0_), channel_id=1, source_target_pairs={{0,8},{1,9},{2,10},{3,11},{4,12},{5,13},{6,14},{7,15},{8,0},{9,1},... | collective-permute-start | bytes 9437192 | tf_op jit(solution)/shard_map/ppermute | solution.py:615
  297.4 135.3 %collective-permute-start.4 = (bf16[384,4096]{1,0:T(8,128)(2,1)}, bf16[384,4096]{1,0:T(8,128)(2,1)}, u32[]{:S(2)}, u32[]{:S(2)}) collective-permute-start(bf16[384,4096]{1,0:T(8,128)(2,1)} %get-tuple-element.48.refs_0_), channel_id=1, source_target_pairs={{0,2},{1,3},{2,0},{3,1},{4,6},{5,7},{6,4},{7,5},{8,10},{9,11},{10,... | collective-permute-start | bytes 9437192 | tf_op jit(solution)/shard_map/ppermute | solution.py:615
  365.8 69.4 %collective-permute-start.5 = (bf16[384,4096]{1,0:T(8,128)(2,1)}, bf16[384,4096]{1,0:T(8,128)(2,1)}, u32[]{:S(2)}, u32[]{:S(2)}) collective-permute-start(bf16[384,4096]{1,0:T(8,128)(2,1)} %get-tuple-element.48.refs_0_), channel_id=1, source_target_pairs={{0,4},{1,5},{2,6},{3,7},{4,0},{5,1},{6,2},{7,3},{8,12},{9,13},{10,... | collective-permute-start | bytes 9437192 | tf_op jit(solution)/shard_map/ppermute | solution.py:615
  366.6 69.1 %collective-permute-start.6 = (bf16[384,4096]{1,0:T(8,128)(2,1)}, bf16[384,4096]{1,0:T(8,128)(2,1)}, u32[]{:S(2)}, u32[]{:S(2)}) collective-permute-start(bf16[384,4096]{1,0:T(8,128)(2,1)} %get-tuple-element.48.refs_0_), channel_id=1, source_target_pairs={{0,8},{1,9},{2,10},{3,11},{4,12},{5,13},{6,14},{7,15},{8,0},{9,1},... | collective-permute-start | bytes 9437192 | tf_op jit(solution)/shard_map/ppermute | solution.py:615
  427.9 147.7 %collective-permute-start.16 = (f32[1536,3072]{1,0:T(8,128)}, f32[1536,3072]{1,0:T(8,128)}, u32[]{:S(2)}, u32[]{:S(2)}) collective-permute-start(f32[1536,3072]{1,0:T(8,128)} %get-tuple-element.62), channel_id=1, source_target_pairs={{0,1},{1,0},{2,3},{3,2},{4,5},{5,4},{6,7},{7,6},{8,9},{9,8},{10,11... | collective-permute-start | bytes 56623112 | tf_op jit(solution)/shard_map/ppermute | solution.py:615
  503.2 72.4 %collective-permute-start.17 = (f32[1536,3072]{1,0:T(8,128)}, f32[1536,3072]{1,0:T(8,128)}, u32[]{:S(2)}, u32[]{:S(2)}) collective-permute-start(f32[1536,3072]{1,0:T(8,128)} %get-tuple-element.63), channel_id=1, source_target_pairs={{0,1},{1,0},{2,3},{3,2},{4,5},{5,4},{6,7},{7,6},{8,9},{9,8},{10,11... | collective-permute-start | bytes 56623112 | tf_op jit(solution)/shard_map/ppermute | solution.py:615
  503.3 70.8 %collective-permute-start.8 = (bf16[384,4096]{1,0:T(8,128)(2,1)}, bf16[384,4096]{1,0:T(8,128)(2,1)}, u32[]{:S(2)}, u32[]{:S(2)}) collective-permute-start(bf16[384,4096]{1,0:T(8,128)(2,1)} %get-tuple-element.54.refs_0_.refs_4_.refs_8_.refs_12_), channel_id=1, source_target_pairs={{0,2},{1,3},{2,0},{3,1},{4,6},{5,7},{6,4},{7,5},{8,10},{9,11},{10,... | collective-permute-start | bytes 9437192 | tf_op jit(solution)/shard_map/ppermute | solution.py:615
  504.5 70.5 %collective-permute-start.9 = (bf16[384,4096]{1,0:T(8,128)(2,1)}, bf16[384,4096]{1,0:T(8,128)(2,1)}, u32[]{:S(2)}, u32[]{:S(2)}) collective-permute-start(bf16[384,4096]{1,0:T(8,128)(2,1)} %get-tuple-element.54.refs_0_.refs_4_.refs_8_.refs_12_), channel_id=1, source_target_pairs={{0,4},{1,5},{2,6},{3,7},{4,0},{5,1},{6,2},{7,3},{8,12},{9,13},{10,... | collective-permute-start | bytes 9437192 | tf_op jit(solution)/shard_map/ppermute | solution.py:615
  505.4 70.2 %collective-permute-start.10 = (bf16[384,4096]{1,0:T(8,128)(2,1)}, bf16[384,4096]{1,0:T(8,128)(2,1)}, u32[]{:S(2)}, u32[]{:S(2)}) collective-permute-start(bf16[384,4096]{1,0:T(8,128)(2,1)} %get-tuple-element.54.refs_0_.refs_4_.refs_8_.refs_12_), channel_id=1, source_target_pairs={{0,8},{1,9},{2,10},{3,11},{4,12},{5,13},{6,14},{7,15},{8,0},{9,1},... | collective-permute-start | bytes 9437192 | tf_op jit(solution)/shard_map/ppermute | solution.py:615
  629.8 77.1 %collective-permute-start.18 = (f32[1152,3072]{1,0:T(8,128)}, f32[1152,3072]{1,0:T(8,128)}, u32[]{:S(2)}, u32[]{:S(2)}) collective-permute-start(f32[1152,3072]{1,0:T(8,128)} %get-tuple-element.67), channel_id=1, source_target_pairs={{0,1},{1,0},{2,3},{3,2},{4,5},{5,4},{6,7},{7,6},{8,9},{9,8},{10,11... | collective-permute-start | bytes 42467336 | tf_op jit(solution)/shard_map/ppermute | solution.py:615
  629.8 70.3 %collective-permute-start.3 = (f32[256,3072]{1,0:T(8,128)}, f32[256,3072]{1,0:T(8,128)}, u32[]{:S(2)}, u32[]{:S(2)}) collective-permute-start(f32[256,3072]{1,0:T(8,128)} %get-tuple-element.47), channel_id=1, source_target_pairs={{0,1},{1,0},{2,3},{3,2},{4,5},{5,4},{6,7},{7,6},{8,9},{9,8},{10,11... | collective-permute-start | bytes 9437192 | tf_op jit(solution)/shard_map/ppermute | solution.py:615
  651.9 26.6 %collective-permute-start.11 = (f32[256,3072]{1,0:T(8,128)}, f32[256,3072]{1,0:T(8,128)}, u32[]{:S(2)}, u32[]{:S(2)}) collective-permute-start(f32[256,3072]{1,0:T(8,128)} %get-tuple-element.58), channel_id=1, source_target_pairs={{0,1},{1,0},{2,3},{3,2},{4,5},{5,4},{6,7},{7,6},{8,9},{9,8},{10,11... | collective-permute-start | bytes 9437192 | tf_op jit(solution)/shard_map/ppermute | solution.py:615
  674.5 44.7 %collective-permute-start.19 = (f32[384,3072]{1,0:T(8,128)}, f32[384,3072]{1,0:T(8,128)}, u32[]{:S(2)}, u32[]{:S(2)}) collective-permute-start(f32[384,3072]{1,0:T(8,128)} %get-tuple-element.68), channel_id=1, source_target_pairs={{0,1},{1,0},{2,3},{3,2},{4,5},{5,4},{6,7},{7,6},{8,9},{9,8},{10,11... | collective-permute-start | bytes 14155784 | tf_op jit(solution)/shard_map/ppermute | solution.py:615
  686.4 1.5 collective-permute-start.12
  688.8 4.9 collective-permute-start.13
  693.7 4.7 collective-permute-start.14
  699.0 5.5 collective-permute-start.15

commit v3 on v2

--- a/solution.py
+++ b/solution.py
@@ -428,13 +428,12 @@
 
 
 BD = 256
-SPLIT = 3
-
-
-def dw_kernel(t, groups, n_in, rows_at, puts, times, tbl, x0, x1, *refs):
+
+
+def dw_kernel(t, n_in, parts, rows_at, puts, tbl, x0, x1, *refs):
     pieces = refs[:4]
     outs = refs[n_in:]
-    buf_ref, ex_ref = outs[:2]
+    buf_ref, *ex_refs = outs[:1 + len(parts)]
     lhs_ref, own_ref, sem, own_sem, ex_sem, put_sem = outs[-6:]
     j = pl.program_id(0)
     core = tbl[0]
@@ -442,23 +441,22 @@
 
     @pl.when(j == 0)
     def _():
-        for wait in (False, True):
-            for s, piece in enumerate(pieces):
-                place = tbl[3 + s] - groups[0]
-
-                @pl.when(jnp.logical_and(place >= 0, tbl[3 + s] < groups[1]))
-                def _():
-                    run_all([pltpu.make_async_copy(piece, lhs_ref.at[aligned(place * GR, GR)], sem.at[s])], wait)
+        copies = [pltpu.make_async_copy(p, lhs_ref.at[my_group(tbl, s)], sem.at[s]) for s, p in enumerate(pieces)]
+        run_all(copies)
+        run_all(copies, True)
 
     def columns(step):
         return aligned(step * BD, BD)
 
-    def own_out(step):
+    def own_out(step, wait=False):
         src = own_ref.at[step % 2]
-        start = (2 * t + core) * CR + groups[0] * GR
-        rows = pl.ds(pl.multiple_of(start, GR), own_ref.shape[1])
-        return (pltpu.make_async_copy(src, buf_ref.at[rows, columns(step)], own_sem.at[step % 2]),
-                pltpu.make_async_copy(src, ex_ref.at[:, columns(step)], ex_sem.at[step % 2]))
+        run_all([pltpu.make_async_copy(
+            src, buf_ref.at[aligned((2 * t + core) * CR, CR), columns(step)], own_sem.at[step % 2])], wait)
+        for (start, stop), ex_ref in zip(parts, ex_refs):
+            @pl.when(jnp.logical_and(step * BD >= start, step * BD < stop))
+            def _():
+                cols = columns(step - start // BD)
+                run_all([pltpu.make_async_copy(src, ex_ref.at[:, cols], ex_sem.at[step % 2])], wait)
 
     put_copies = []
     for n, (at, row_block) in enumerate(puts):
@@ -468,17 +466,13 @@
 
     x = jnp.concatenate([ref[0, r] for ref in (x0, x1) for r in range(NDEV)], axis=0)
     res = dot_nn(lhs_ref[...], x)
-    if times is not None:
-        part = dot_nn(extra[0][...], extra[1][...])
-        for k in range(2):
-            outs[times + k][...] = part[k * B * TOK:(k + 1) * B * TOK]
 
     @pl.when(j >= 2)
     def _():
-        run_all(own_out(j - 2), True)
+        own_out(j - 2, True)
 
     own_ref[j % 2] = res
-    run_all(own_out(j))
+    own_out(j)
 
     if rows_at is not None:
         @pl.when(j == 0)
@@ -491,28 +485,21 @@
 
     @pl.when(j == pl.num_programs(0) - 1)
     def _():
-        run_all(own_out(j - 1) + own_out(j), True)
-
-
-def weight_grad(tbl, gathered, pieces, t, which, out_rows, prev=None, rows=True, puts=(), times=None, groups=(0, 4)):
-    n_rows = (groups[1] - groups[0]) * GR
+        own_out(j - 1, True)
+        own_out(j, True)
+
+
+def weight_grad(tbl, gathered, pieces, t, which, out_rows, prev=None, rows=True, puts=(), parts=((0, D),)):
     anywhere = pl.BlockSpec(memory_space=pl.ANY)
     x_spec = lambda b: pl.BlockSpec((1, NDEV, TOK, BD), lambda j, t: (b, 0, which, j))
     ins = [(x_spec(b), gathered) for b in range(B)] + [(anywhere, p) for p in pieces]
-    outs = [(anywhere, (out_rows, D), F32), (anywhere, (n_rows, D), F32)]
-    rows_at = times_at = None
+    outs = [(anywhere, (out_rows, D), F32)] + [(anywhere, (CR, stop - start), F32) for start, stop in parts]
+    rows_at = None
     put_at = []
-    whole = fixed(2 * B * TOK, CR)
     if rows:
         rows_at = len(outs)
-        outs.append((whole, (2 * B * TOK, CR), BF16))
-    if times is not None:
-        times_at = len(outs)
-        outs += [(by_column(B * TOK, BD), (B * TOK, D), F32)] * 2
+        outs.append((fixed(2 * B * TOK, CR), (2 * B * TOK, CR), BF16))
     ins += [(by_column(CR, BD), block) for block, *_ in puts]
-    if times is not None:
-        ins.append((whole, times[0]))
-        ins.append((pl.BlockSpec((CR, BD), lambda j, t: (2 * times[2] + t[0], j)), times[1]))
     alias = {}
     if prev is not None:
         alias[1 + len(ins)] = 0
@@ -524,21 +511,21 @@
             ins.append((anywhere, buffer))
             outs.append((anywhere, buffer.shape, F32))
     return pl.pallas_call(
-        functools.partial(dw_kernel, t, groups, len(ins) - B, rows_at, put_at, times_at),
+        functools.partial(dw_kernel, t, len(ins) - B, parts, rows_at, put_at),
         grid_spec=pltpu.PrefetchScalarGridSpec(
             num_scalar_prefetch=1,
             grid=(D // BD,),
             in_specs=[spec for spec, _ in ins],
             out_specs=[spec for spec, *_ in outs],
             scratch_shapes=[
-                pltpu.VMEM((n_rows, B * S), BF16),
-                pltpu.VMEM((2, n_rows, BD), F32),
+                pltpu.VMEM((CR, B * S), BF16),
+                pltpu.VMEM((2, CR, BD), F32),
                 dma((4,)), dma((2,)), dma((2,)), dma((2,)),
             ]),
         out_shape=[jax.ShapeDtypeStruct(*shape) for _, *shape in outs],
         input_output_aliases=alias,
         compiler_params=params(),
-        cost_estimate=cost(2 * n_rows * D * B * S, 75e6),
+        cost_estimate=cost(2 * CR * D * B * S, 75e6),
         name="weight_grad",
     )(tbl, *(arg for _, arg in ins))
 
@@ -550,11 +537,13 @@
     rows = jnp.concatenate([r[...] for r in refs[1:1 + n]], axis=1)
     weight = jnp.concatenate([r[...] for r in refs[1 + n:1 + 2 * n]], axis=0)
     acc = dot_nn(rows, weight)
-    for k, prev in enumerate(refs[1 + 2 * n:-2]):
-        refs[k - 2][...] = acc[k * B * TOK:(k + 1) * B * TOK] + prev[...]
-
-
-def contract(tbl, rows, weight, blocks, prev):
+    prev = refs[1 + 2 * n:-2]
+    for k in range(2):
+        part = acc[k * B * TOK:(k + 1) * B * TOK]
+        refs[k - 2][...] = part + prev[k][...] if prev else part
+
+
+def contract(tbl, rows, weight, blocks, prev=()):
     out = by_column(B * TOK, CB)
     w_spec = lambda block: pl.BlockSpec((CR, CB), lambda i, t: (2 * block + t[0], i))
     n = len(blocks)
@@ -564,7 +553,7 @@
             num_scalar_prefetch=1,
             grid=(D // CB,),
             in_specs=[fixed(2 * B * TOK, CR)] * n
-            + [w_spec(block) for block in blocks] + [out] * 2,
+            + [w_spec(block) for block in blocks] + [out] * len(prev),
             out_specs=[out] * 2),
         out_shape=[jax.ShapeDtypeStruct((B * TOK, D), F32)] * 2,
         compiler_params=params(),
@@ -637,29 +626,32 @@
         def grad(name, *args, **kw):
             return weight_grad(tbl, gathered, pieces[name[0]], *args, **kw)
 
+        def rows_times(*args):
+            return contract(tbl, *args)
+
         gwo, ex_o, rows_o = grad("o", 0, GY, D)
+        y_own, y_peer = rows_times([rows_o], w_out.reshape(D, D), [0])
+        y_peer = swap(y_peer)
         ex_o = swap(ex_o)
-        gwq, ex_v, rows_v, y_own, y_peer = grad("v", 2, U, 3 * D, times=(rows_o, w_out.reshape(D, D), 0))
-        y_peer = swap(y_peer)
+        gwq, ex_v, rows_v = grad("v", 2, U, 3 * D)
         ex_v = swap(ex_v)
-        gwq, ex_k, rows_k, *du, gwo = grad("k", 1, U, 3 * D, gwq, puts=[(ex_o, 0, gwo)], times=(rows_v, flat_w, 2))
+        du = rows_times([rows_v], flat_w, [2])
+        gwq, ex_k, rows_k, gwo = grad("k", 1, U, 3 * D, gwq, puts=[(ex_o, 0, gwo)])
+        ex_k = swap(ex_k)
         rows_q = collect(tbl, pieces["q"])
-        ex_k = swap(ex_k)
-        du_own, du_peer = contract(tbl, [rows_k, rows_q], flat_w, [1, 0], du)
+        du_own, du_peer = rows_times([rows_k, rows_q], flat_w, [1, 0], du)
         du_peer = swap(du_peer)
+        parts = ((0, 2 * D // 3), (2 * D // 3, D))
+        gwq, *ex_q = grad("q", 0, U, 3 * D, gwq, rows=False, puts=[(ex_v, 2, None), (ex_k, 1, None)], parts=parts)
+        ex_q = [swap(ex) for ex in ex_q]
         y_out, = finish(finish_y_kernel, [y_own, y_peer], [x_in], b_out)
         db = jnp.where(chip < 4, db[0, :, :, 0] + db[1, :, :, 0], 0.0).reshape(3, 1, GR)
         sums = lax.dynamic_update_slice(jnp.zeros((8, 8, GR), F32), db, (3, mine, 0)).reshape(8, D)
         grad_x, sums = finish(finish_kernel, [du_own, du_peer], [x_in, grad_y], ln_gain, sums)
-        parts = [(0, SPLIT), (SPLIT, 4)]
-        gwq, ex_q0 = grad("q0", 0, U, 3 * D, gwq, rows=False, puts=[(ex_v, 2, None), (ex_k, 1, None)], groups=parts[0])
-        ex_q0 = swap(ex_q0)
-        gwq, ex_q1 = grad("q1", 0, U, 3 * D, gwq, rows=False, groups=parts[1])
-        ex_q1 = swap(ex_q1)
-        for bit in (1, *NEAR):
+        for bit in (*NEAR, 1):
             sums = sums + permute(sums, bit)
-        for ex, part in ((ex_q0, parts[0]), (ex_q1, parts[1])):
-            gwq = lax.dynamic_update_slice(gwq, ex, ((1 - core) * CR + part[0] * GR, 0))
+        for n, ex in enumerate(ex_q):
+            gwq = lax.dynamic_update_slice(gwq, ex, ((1 - core) * CR, parts[n][0]))
 
         grad_w_qkv = jnp.transpose(gwq.reshape(3, NH, DH, D), (3, 0, 1, 2))
         grad_b_qkv = sums[3:6].reshape(3, NH, DH)

time: 725 us -> 728 us (level)
  waiting for transfers between devices: 153 us -> 161 us
    pallas_call x5 -> x4, Pallas kernels: 258 us -> 230 us  [weight_grad(): pl.pallas_call(functools.partial(dw_kernel, t, len(ins) - B, parts, rows_...]
    pallas_call x1 -> x3, Pallas kernels: 17.8 us -> 40.1 us  [contract(): pl.pallas_call(functools.partial(contract_kernel, n), grid_spec=pltpu.Pre...]
    ppermute x20, waiting for transfers between devices: 153 us -> 161 us  [permute(): return lax.ppermute(a, 'sp', [(i, i ^ bit) for i in range(NDEV)])]
  transfers between devices with their start and end apart: 20 -> 20, of which waited for: 10 -> 10; matrix products, arithmetic and copies ran while one was open for 3% -> 3% of each run, Pallas kernels for 25% -> 23%
where the time goes in v3:
time: 728 us; the launch traced here: 727 us
  Pallas kernels  523 us (72%)
  waiting for transfers between devices  161 us (22%)
  local copies, waits for them, and re-layouts  24 us (3%)
  starting transfers between devices  14 us (2%)
    pallas_call x1, Pallas kernels, front(): pl.pallas_call(front_kernel, in_specs=[vmem, anywhere, vmem, vmem, anywhe...  237 us
    pallas_call x4, Pallas kernels, weight_grad(): pl.pallas_call(functools.partial(dw_kernel, t, len(ins) - B, parts, rows_...  230 us
    ppermute x20, waiting for transfers between devices, permute(): return lax.ppermute(a, 'sp', [(i, i ^ bit) for i in range(NDEV)])  161 us
    pallas_call x3, Pallas kernels, contract(): pl.pallas_call(functools.partial(contract_kernel, n), grid_spec=pltpu.Pre...  40.1 us
    dynamic_update_slice x2, local copies, waits for them, and re-layouts, block(): gwq = lax.dynamic_update_slice(gwq, ex, ((1 - core) * CR, parts[n][0]))  18.2 us
  transfers between devices with their start and end apart: 20, of which 10 were waited for; matrix products, arithmetic and copies ran while one was open for 3% of the time, Pallas kernels for 23%

profile of v3, /device:TPU:0, one launch (start us, length us, event | category | flops | bytes accessed | tf_op | source)
XLA Modules:
  0.0 726.9 jit_solution(5084882367959526209)
XLA Ops:
  0.7 0.9 reshape.81
  1.6 1.1 copy.24.refs_6_
  2.6 0.6 stack.31.tbl.refs_0_
  3.2 236.9 %front.1 = (bf16[2,16,256,3072]{3,2,1,0:T(8,128)(2,1)}, bf16[384,4096]{1,0:T(8,128)(2,1)}, bf16[384,4096]{1,0:T(8,128)(2,1)}, bf16[384,4096]{1,0:T(8,128)(2,1)},...) custom-call(bf16[2,128,3072]{2,1,0:T(8,128)(2,1)} %x_ref.3, ...), custom_call_target="tpu_custom_call" | custom-call | flops 149999992832 | bytes 200000000 | tf_op jit(solution)/shard_map/front/pallas_call | solution.py:375
  240.2 54.0 %weight_grad.4 = (f32[3072,3072]{1,0:T(8,128)}, f32[1536,3072]{1,0:T(8,128)}, bf16[512,1536]{1,0:T(8,128)(2,1)}) custom-call(s32[7]{0:T(128)} %stack.31.tbl.refs_0_, bf16[2,16,256,3072]{3,2,1,0:T(8,128)(2,1)} %get-tuple-element.38.x0.x1, bf16[2,16,256,3072]{3,2,1,0:T(8,128)(2,1)} %get-tuple-element.38.x0.x1, bf16[384,4096]{1,0:T(8,128)(2,1)} %get-tuple-element.39.refs_0_, ...), custom_call_target="tpu_custom_call" | custom-call | flops 38654705664 | bytes 75000000 | tf_op jit(solution)/shard_map/weight_grad/pallas_call | solution.py:513
  294.2 0.9 collective-permute-start.5
  295.1 1.2 collective-permute-start.6
  296.2 0.9 collective-permute-start.7
  297.1 1.1 collective-permute-start.1
  298.2 67.3 %collective-permute-done.5.refs_1_ = bf16[384,4096]{1,0:T(8,128)(2,1)} collective-permute-done((bf16[384,4096]{1,0:T(8,128)(2,1)}, bf16[384,4096]{1,0:T(8,128)(2,1)}, u32[]{:S(2)}, u32[]{:S(2)}) %collective-permute-start.5) | collective-permute-done | bytes 3145760 | tf_op jit(solution)/shard_map/ppermute | solution.py:604
  365.5 0.8 collective-permute-start.2
  366.3 1.2 collective-permute-start.3
  367.5 53.8 %weight_grad.5 = (f32[9216,3072]{1,0:T(8,128)}, f32[1536,3072]{1,0:T(8,128)}, bf16[512,1536]{1,0:T(8,128)(2,1)}) custom-call(s32[7]{0:T(128)} %stack.31.tbl.refs_0_, bf16[2,16,256,3072]{3,2,1,0:T(8,128)(2,1)} %get-tuple-element.38.x0.x1, bf16[2,16,256,3072]{3,2,1,0:T(8,128)(2,1)} %get-tuple-element.38.x0.x1, bf16[384,4096]{1,0:T(8,128)(2,1)} %get-tuple-element.48.refs_0_, ...), custom_call_target="tpu_custom_call" | custom-call | flops 38654705664 | bytes 75000000 | tf_op jit(solution)/shard_map/weight_grad/pallas_call | solution.py:513
  421.3 11.1 %collective-permute-done.1.refs_1_ = bf16[384,4096]{1,0:T(8,128)(2,1)} collective-permute-done((bf16[384,4096]{1,0:T(8,128)(2,1)}, bf16[384,4096]{1,0:T(8,128)(2,1)}, u32[]{:S(2)}, u32[]{:S(2)}) %collective-permute-start.1) | collective-permute-done | bytes 3145760 | tf_op jit(solution)/shard_map/ppermute | solution.py:604
  432.4 2.5 collective-permute-done.2.refs_2_
  434.9 0.6 collective-permute-done.3.refs_3_
  435.5 58.1 %weight_grad.6 = (f32[9216,3072]{1,0:T(8,128)}, f32[1536,3072]{1,0:T(8,128)}, bf16[512,1536]{1,0:T(8,128)(2,1)}, f32[3072,3072]{1,0:T(8,128)}) custom-call(s32[7]{0:T(128)} %stack.31.tbl.refs_0_, bf16[2,16,256,3072]{3,2,1,0:T(8,128)(2,1)} %get-tuple-element.38.x0.x1, ...), custom_call_target="tpu_custom_call", output_to_operand_aliasing={{0}: (8, {}), {3}: (9, {})} | custom-call | flops 38654705664 | bytes 75000000 | tf_op jit(solution)/shard_map/weight_grad/pallas_call | solution.py:513
  493.7 1.2 collective-permute-start.8
  494.9 0.9 collective-permute-start.9
  495.8 1.2 collective-permute-start.10
  496.9 67.6 %collective-permute-done.8.refs_1_.refs_5_.refs_9_.refs_13_ = bf16[384,4096]{1,0:T(8,128)(2,1)} collective-permute-done((bf16[384,4096]{1,0:T(8,128)(2,1)}, bf16[384,4096]{1,0:T(8,128)(2,1)}, u32[]{:S(2)}, u32[]{:S(2)}) %collective-permute-start.8) | collective-permute-done | bytes 3145760 | tf_op jit(solution)/shard_map/ppermute | solution.py:604
  564.5 0.9 collective-permute-done.9.refs_2_.refs_6_.refs_10_.refs_14_
  565.4 0.6 collective-permute-done.10.refs_3_.refs_7_.refs_11_.refs_15_
  566.0 63.9 %weight_grad.7 = (f32[9216,3072]{1,0:T(8,128)}, f32[1536,2048]{1,0:T(8,128)}, f32[1536,1024]{1,0:T(8,128)}) custom-call(s32[7]{0:T(128)} %stack.31.tbl.refs_0_, bf16[2,16,256,3072]{3,2,1,0:T(8,128)(2,1)} %get-tuple-element.38.x0.x1, bf16[2,16,256,3072]{3,2,1,0:T(8,128)(2,1)} %get-tuple-element.38.x0.x1, ...), custom_call_target="tpu_custom_call", output_to_operand_aliasing={{0}: (9, {})} | custom-call | flops 38654705664 | bytes 75000000 | tf_op jit(solution)/shard_map/weight_grad/pallas_call | solution.py:513
  629.9 0.5 collective-permute-start.19
  630.4 11.2 %contract.4 = (f32[256,3072]{1,0:T(8,128)}, f32[256,3072]{1,0:T(8,128)}) custom-call(s32[7]{0:T(128)} %stack.31.tbl.refs_0_, bf16[512,1536]{1,0:T(8,128)(2,1)} %get-tuple-element.53.refs_1_, bf16[9216,3072]{1,0:T(8,128)(2,1)} %bitcast.28), custom_call_target="tpu_custom_call" | custom-call | flops 4831838208 | bytes 22000000 | tf_op jit(solution)/shard_map/contract/pallas_call | solution.py:550
  641.6 3.8 collect.1.refs_2_
  645.3 17.7 %contract.5 = (f32[256,3072]{1,0:T(8,128)}, f32[256,3072]{1,0:T(8,128)}) custom-call(s32[7]{0:T(128)} %stack.31.tbl.refs_0_, bf16[512,1536]{1,0:T(8,128)(2,1)} %get-tuple-element.51.refs_1_, bf16[512,1536]{1,0:T(8,128)(2,1)} %collect.1.refs_2_, bf16[9216,3072]{1,0:T(8,128)(2,1)} %bitcast.29, bf16[9216,3072]{1,0:T(8,128)(2,1)} %bitcast.30, ...), custom_call_target="tpu_custom_call" | custom-call | flops 9663676416 | bytes 22000000 | tf_op jit(solution)/shard_map/contract/pallas_call | solution.py:550
  663.1 11.2 %contract.3 = (f32[256,3072]{1,0:T(8,128)}, f32[256,3072]{1,0:T(8,128)}) custom-call(s32[7]{0:T(128)} %stack.31.tbl.refs_0_, bf16[512,1536]{1,0:T(8,128)(2,1)} %get-tuple-element.43.refs_1_, bf16[3072,3072]{1,0:T(8,128)(2,1)} %bitcast.33), custom_call_target="tpu_custom_call" | custom-call | flops 4831838208 | bytes 22000000 | tf_op jit(solution)/shard_map/contract/pallas_call | solution.py:550
  674.3 0.5 collective-permute-start
  674.7 1.5 select_reduce_fusion
  676.2 0.6 broadcast_in_dim.7
  676.9 1.3 dynamic_update_slice.9
  678.2 8.0 %finish.3 = (bf16[2,128,3072]{2,1,0:T(8,128)(2,1)}, f32[8,3072]{1,0:T(8,128)}) custom-call(f32[256,3072]{1,0:T(8,128)} %get-tuple-element.56.du_own, f32[256,3072]{1,0:T(8,128)} %collective-permute-done.11.du_peer, bf16[2,128,3072]{2,1,0:T(8,128)(2,1)} %x_ref.3, bf16[2,128,3072]{2,1,0:T(8,128)(2,1)} %gy_ref.1, f32[8,3072]{1,0:T(8,128)} %bitcast.16.db_ref, ...), custom_call_target="tpu_custom_call" | custom-call | flops 100000000 | bytes 10000000 | tf_op jit(solution)/shard_map/finish/pallas_call | solution.py:589
  686.2 1.2 collective-permute-start.12
  687.3 3.8 collective-permute-done.12
  691.1 0.9 add.43
  692.0 1.2 collective-permute-start.13
  693.2 3.5 collective-permute-done.13
  696.7 1.2 collective-permute-start.14
  697.9 3.5 collective-permute-done.14
  701.4 0.6 add.45
  702.0 4.4 finish.2
  706.4 1.0 add.46
  707.4 0.7 reshape.88
  708.1 0.6 fusion
  708.7 11.5 %constant_dynamic-update-slice_fusion.1 = f32[9216,3072]{1,0:T(8,128)} fusion(f32[9216,3072]{1,0:T(8,128)} %get-tuple-element.64, f32[1536,2048]{1,0:T(8,128)} %collective-permute-done.18, s32[]{:T(128)S(6)} %select_n.59), kind=kLoop, calls=%fused_computation.2 | loop fusion | bytes 25165828 | tf_op jit(solution)/shard_map/dynamic_update_slice | solution.py:654
  720.3 6.6 constant_dynamic-update-slice_fusion
  (19 shorter events, 0.3 us)
Async XLA Ops:
  294.1 141.4 %collective-permute-start.4 = (f32[1536,3072]{1,0:T(8,128)}, f32[1536,3072]{1,0:T(8,128)}, u32[]{:S(2)}, u32[]{:S(2)}) collective-permute-start(f32[1536,3072]{1,0:T(8,128)} %get-tuple-element.47), channel_id=1, source_target_pairs={{0,1},{1,0},{2,3},{3,2},{4,5},{5,4},{6,7},{7,6},{8,9},{9,8},{10,11... | collective-permute-start | bytes 56623112 | tf_op jit(solution)/shard_map/ppermute | solution.py:604
  294.2 71.3 %collective-permute-start.5 = (bf16[384,4096]{1,0:T(8,128)(2,1)}, bf16[384,4096]{1,0:T(8,128)(2,1)}, u32[]{:S(2)}, u32[]{:S(2)}) collective-permute-start(bf16[384,4096]{1,0:T(8,128)(2,1)} %get-tuple-element.48.refs_0_), channel_id=1, source_target_pairs={{0,2},{1,3},{2,0},{3,1},{4,6},{5,7},{6,4},{7,5},{8,10},{9,11},{10,... | collective-permute-start | bytes 9437192 | tf_op jit(solution)/shard_map/ppermute | solution.py:604
  295.1 71.3 %collective-permute-start.6 = (bf16[384,4096]{1,0:T(8,128)(2,1)}, bf16[384,4096]{1,0:T(8,128)(2,1)}, u32[]{:S(2)}, u32[]{:S(2)}) collective-permute-start(bf16[384,4096]{1,0:T(8,128)(2,1)} %get-tuple-element.48.refs_0_), channel_id=1, source_target_pairs={{0,4},{1,5},{2,6},{3,7},{4,0},{5,1},{6,2},{7,3},{8,12},{9,13},{10,... | collective-permute-start | bytes 9437192 | tf_op jit(solution)/shard_map/ppermute | solution.py:604
  296.2 71.3 %collective-permute-start.7 = (bf16[384,4096]{1,0:T(8,128)(2,1)}, bf16[384,4096]{1,0:T(8,128)(2,1)}, u32[]{:S(2)}, u32[]{:S(2)}) collective-permute-start(bf16[384,4096]{1,0:T(8,128)(2,1)} %get-tuple-element.48.refs_0_), channel_id=1, source_target_pairs={{0,8},{1,9},{2,10},{3,11},{4,12},{5,13},{6,14},{7,15},{8,0},{9,1},... | collective-permute-start | bytes 9437192 | tf_op jit(solution)/shard_map/ppermute | solution.py:604
  297.1 135.3 %collective-permute-start.1 = (bf16[384,4096]{1,0:T(8,128)(2,1)}, bf16[384,4096]{1,0:T(8,128)(2,1)}, u32[]{:S(2)}, u32[]{:S(2)}) collective-permute-start(bf16[384,4096]{1,0:T(8,128)(2,1)} %get-tuple-element.46.refs_0_), channel_id=1, source_target_pairs={{0,2},{1,3},{2,0},{3,1},{4,6},{5,7},{6,4},{7,5},{8,10},{9,11},{10,... | collective-permute-start | bytes 9437192 | tf_op jit(solution)/shard_map/ppermute | solution.py:604
  365.5 69.4 %collective-permute-start.2 = (bf16[384,4096]{1,0:T(8,128)(2,1)}, bf16[384,4096]{1,0:T(8,128)(2,1)}, u32[]{:S(2)}, u32[]{:S(2)}) collective-permute-start(bf16[384,4096]{1,0:T(8,128)(2,1)} %get-tuple-element.46.refs_0_), channel_id=1, source_target_pairs={{0,4},{1,5},{2,6},{3,7},{4,0},{5,1},{6,2},{7,3},{8,12},{9,13},{10,... | collective-permute-start | bytes 9437192 | tf_op jit(solution)/shard_map/ppermute | solution.py:604
  366.3 69.1 %collective-permute-start.3 = (bf16[384,4096]{1,0:T(8,128)(2,1)}, bf16[384,4096]{1,0:T(8,128)(2,1)}, u32[]{:S(2)}, u32[]{:S(2)}) collective-permute-start(bf16[384,4096]{1,0:T(8,128)(2,1)} %get-tuple-element.46.refs_0_), channel_id=1, source_target_pairs={{0,8},{1,9},{2,10},{3,11},{4,12},{5,13},{6,14},{7,15},{8,0},{9,1},... | collective-permute-start | bytes 9437192 | tf_op jit(solution)/shard_map/ppermute | solution.py:604
  421.3 144.7 %collective-permute-start.16 = (f32[1536,3072]{1,0:T(8,128)}, f32[1536,3072]{1,0:T(8,128)}, u32[]{:S(2)}, u32[]{:S(2)}) collective-permute-start(f32[1536,3072]{1,0:T(8,128)} %get-tuple-element.61), channel_id=1, source_target_pairs={{0,1},{1,0},{2,3},{3,2},{4,5},{5,4},{6,7},{7,6},{8,9},{9,8},{10,11... | collective-permute-start | bytes 56623112 | tf_op jit(solution)/shard_map/ppermute | solution.py:604
  493.6 72.4 %collective-permute-start.17 = (f32[1536,3072]{1,0:T(8,128)}, f32[1536,3072]{1,0:T(8,128)}, u32[]{:S(2)}, u32[]{:S(2)}) collective-permute-start(f32[1536,3072]{1,0:T(8,128)} %get-tuple-element.62), channel_id=1, source_target_pairs={{0,1},{1,0},{2,3},{3,2},{4,5},{5,4},{6,7},{7,6},{8,9},{9,8},{10,11... | collective-permute-start | bytes 56623112 | tf_op jit(solution)/shard_map/ppermute | solution.py:604
  493.7 70.8 %collective-permute-start.8 = (bf16[384,4096]{1,0:T(8,128)(2,1)}, bf16[384,4096]{1,0:T(8,128)(2,1)}, u32[]{:S(2)}, u32[]{:S(2)}) collective-permute-start(bf16[384,4096]{1,0:T(8,128)(2,1)} %get-tuple-element.52.refs_0_.refs_4_.refs_8_.refs_12_), channel_id=1, source_target_pairs={{0,2},{1,3},{2,0},{3,1},{4,6},{5,7},{6,4},{7,5},{8,10},{9,11},{10,... | collective-permute-start | bytes 9437192 | tf_op jit(solution)/shard_map/ppermute | solution.py:604
  494.9 70.5 %collective-permute-start.9 = (bf16[384,4096]{1,0:T(8,128)(2,1)}, bf16[384,4096]{1,0:T(8,128)(2,1)}, u32[]{:S(2)}, u32[]{:S(2)}) collective-permute-start(bf16[384,4096]{1,0:T(8,128)(2,1)} %get-tuple-element.52.refs_0_.refs_4_.refs_8_.refs_12_), channel_id=1, source_target_pairs={{0,4},{1,5},{2,6},{3,7},{4,0},{5,1},{6,2},{7,3},{8,12},{9,13},{10,... | collective-permute-start | bytes 9437192 | tf_op jit(solution)/shard_map/ppermute | solution.py:604
  495.8 70.2 %collective-permute-start.10 = (bf16[384,4096]{1,0:T(8,128)(2,1)}, bf16[384,4096]{1,0:T(8,128)(2,1)}, u32[]{:S(2)}, u32[]{:S(2)}) collective-permute-start(bf16[384,4096]{1,0:T(8,128)(2,1)} %get-tuple-element.52.refs_0_.refs_4_.refs_8_.refs_12_), channel_id=1, source_target_pairs={{0,8},{1,9},{2,10},{3,11},{4,12},{5,13},{6,14},{7,15},{8,0},{9,1},... | collective-permute-start | bytes 9437192 | tf_op jit(solution)/shard_map/ppermute | solution.py:604
  629.8 78.9 %collective-permute-start.18 = (f32[1536,2048]{1,0:T(8,128)}, f32[1536,2048]{1,0:T(8,128)}, u32[]{:S(2)}, u32[]{:S(2)}) collective-permute-start(f32[1536,2048]{1,0:T(8,128)} %get-tuple-element.65), channel_id=1, source_target_pairs={{0,1},{1,0},{2,3},{3,2},{4,5},{5,4},{6,7},{7,6},{8,9},{9,8},{10,11... | collective-permute-start | bytes 37748744 | tf_op jit(solution)/shard_map/ppermute | solution.py:604
  629.9 90.4 %collective-permute-start.19 = (f32[1536,1024]{1,0:T(8,128)}, f32[1536,1024]{1,0:T(8,128)}, u32[]{:S(2)}, u32[]{:S(2)}) collective-permute-start(f32[1536,1024]{1,0:T(8,128)} %get-tuple-element.66), channel_id=1, source_target_pairs={{0,1},{1,0},{2,3},{3,2},{4,5},{5,4},{6,7},{7,6},{8,9},{9,8},{10,11... | collective-permute-start | bytes 18874376 | tf_op jit(solution)/shard_map/ppermute | solution.py:604
  663.1 15.1 %collective-permute-start.11 = (f32[256,3072]{1,0:T(8,128)}, f32[256,3072]{1,0:T(8,128)}, u32[]{:S(2)}, u32[]{:S(2)}) collective-permute-start(f32[256,3072]{1,0:T(8,128)} %get-tuple-element.57), channel_id=1, source_target_pairs={{0,1},{1,0},{2,3},{3,2},{4,5},{5,4},{6,7},{7,6},{8,9},{9,8},{10,11... | collective-permute-start | bytes 9437192 | tf_op jit(solution)/shard_map/ppermute | solution.py:604
  674.3 27.7 %collective-permute-start = (f32[256,3072]{1,0:T(8,128)}, f32[256,3072]{1,0:T(8,128)}, u32[]{:S(2)}, u32[]{:S(2)}) collective-permute-start(f32[256,3072]{1,0:T(8,128)} %get-tuple-element.45), channel_id=1, source_target_pairs={{0,1},{1,0},{2,3},{3,2},{4,5},{5,4},{6,7},{7,6},{8,9},{9,8},{10,11... | collective-permute-start | bytes 9437192 | tf_op jit(solution)/shard_map/ppermute | solution.py:604
  686.2 5.0 collective-permute-start.12
  692.0 4.7 collective-permute-start.13
  696.7 4.7 collective-permute-start.14
  702.0 4.4 collective-permute-start.15

commit v4 on v3

--- a/solution.py
+++ b/solution.py
@@ -136,11 +136,11 @@
 
 
 def front_kernel(*refs):
-    x_ref, gy_ref, gain_ref, lnb_ref, w_ref, wout_ref, bias_ref = refs[:7]
+    x_ref, gy_ref, gain_ref, lnb_ref, w_ref, wout_ref, b_ref = refs[:7]
     all_ref, *piece_refs = refs[7:12]
     far_refs = refs[12:15]
     db_ref = refs[15]
-    (wt_ref, wo_ref, qkv_ref, do_ref, pair_ref, head_ref, u_ref, dk_acc, dv_acc,
+    (bias_ref, wt_ref, wo_ref, qkv_ref, do_ref, pair_ref, head_ref, u_ref, dk_acc, dv_acc,
      send_sem, recv_sem, peer_sem, own_sem, pair_sem, head_sem, w_sem, osend_sem, orecv_sem) = refs[16:]
     me = lax.axis_index("sp")
     near = {bit: flip(me, bit) for bit in NEAR}
@@ -280,8 +280,11 @@
             stage0(0, U)
         stage0_peer(b, U)
         stage0_peer(b, GY)
-    for c in weights:
-        c.wait()
+    on_diagonal = lax.broadcasted_iota(jnp.int32, (DH, DH), 0) == lax.broadcasted_iota(jnp.int32, (DH, DH), 1)
+    for n in range(3 * GH):
+        row = b_ref[n // GH, pl.ds(GH * mine + n % GH, 1), :]
+        bias_ref[n * DH:(n + 1) * DH, :] = jnp.sum(jnp.where(on_diagonal, row, 0.0), **LAST_DIM)
+    run_all(weights, True)
 
     def head_of(ref, i):
         return ref.at[aligned((i % GH) * DH, DH), aligned((i // GH) * S, S)]
@@ -334,8 +337,8 @@
         AT0 + 1: [lambda: stage1(1, GY)],
         AT0 + 2: [lambda: stage1(1, U)],
         NEXT1: [lambda: stage2(1, GY)],
-        15: [lambda: stage2(1, U)],
-        17: [lambda: stage3(1, GY), lambda: stage3(1, U), first_o],
+        15: [lambda: stage2(1, U), first_o],
+        17: [lambda: stage3(1, GY), lambda: stage3(1, U)],
     }
 
     def step(k, carry):
@@ -378,6 +381,7 @@
         out_specs=[anywhere] * 8 + [vmem],
         out_shape=[gathered] + [piece] * 7 + [jax.ShapeDtypeStruct((B, 3, GR, LANES), F32)],
         scratch_shapes=[
+            pltpu.VMEM((3 * GR, 1), F32),
             pltpu.VMEM((3 * GR, D), BF16),
             pltpu.VMEM((GR, D), BF16),
             pltpu.VMEM((B, 3 * GR, S), BF16),
@@ -612,9 +616,8 @@
         mine = 4 * core + groups[0]
 
         flat_w = jnp.transpose(w_qkv, (1, 2, 3, 0)).reshape(3 * D, D)
-        bias = lax.dynamic_slice_in_dim(b_qkv.reshape(3, 8, GR), mine, 1, axis=1).reshape(3 * GR, 1)
         gathered, o, dq, dk, dv, *far_o, db = front(
-            x_in, grad_y, ln_gain, ln_bias, flat_w.reshape(3, 8, GR, D), w_out, bias)
+            x_in, grad_y, ln_gain, ln_bias, flat_w.reshape(3, 8, GR, D), w_out, b_qkv)
 
         pieces = {"o": [o] + far_o}
         for name, piece in (("v", dv), ("k", dk), ("q", dq)):

time: 728 us -> 726 us (level)
  no operation moved by 1% of the time
where the time goes in v4:
time: 726 us; the launch traced here: 725 us
  Pallas kernels  523 us (72%)
  waiting for transfers between devices  161 us (22%)
  local copies, waits for them, and re-layouts  22.1 us (3%)
  starting transfers between devices  14.3 us (2%)
    pallas_call x1, Pallas kernels, front(): pl.pallas_call(front_kernel, in_specs=[vmem, anywhere, vmem, vmem, anywhe...  237 us
    pallas_call x4, Pallas kernels, weight_grad(): pl.pallas_call(functools.partial(dw_kernel, t, len(ins) - B, parts, rows_...  230 us
    ppermute x20, waiting for transfers between devices, permute(): return lax.ppermute(a, 'sp', [(i, i ^ bit) for i in range(NDEV)])  161 us
    pallas_call x3, Pallas kernels, contract(): pl.pallas_call(functools.partial(contract_kernel, n), grid_spec=pltpu.Pre...  40.1 us
    dynamic_update_slice x2, local copies, waits for them, and re-layouts, block(): gwq = lax.dynamic_update_slice(gwq, ex, ((1 - core) * CR, parts[n][0]))  18.2 us
  transfers between devices with their start and end apart: 20, of which 10 were waited for; matrix products, arithmetic and copies ran while one was open for 3% of the time, Pallas kernels for 23%

profile of v4, /device:TPU:0, one launch (start us, length us, event | category | flops | bytes accessed | tf_op | source)
XLA Modules:
  0.0 724.7 jit_solution(10099707483584629517)
XLA Ops:
  0.7 0.6 stack.31.tbl.refs_0_
  1.3 236.8 %front.1 = (bf16[2,16,256,3072]{3,2,1,0:T(8,128)(2,1)}, bf16[384,4096]{1,0:T(8,128)(2,1)}, bf16[384,4096]{1,0:T(8,128)(2,1)}, bf16[384,4096]{1,0:T(8,128)(2,1)},...) custom-call(bf16[2,128,3072]{2,1,0:T(8,128)(2,1)} %x_ref.3, ...), custom_call_target="tpu_custom_call" | custom-call | flops 149999992832 | bytes 200000000 | tf_op jit(solution)/shard_map/front/pallas_call | solution.py:378
  238.1 54.0 %weight_grad.4 = (f32[3072,3072]{1,0:T(8,128)}, f32[1536,3072]{1,0:T(8,128)}, bf16[512,1536]{1,0:T(8,128)(2,1)}) custom-call(s32[7]{0:T(128)} %stack.31.tbl.refs_0_, bf16[2,16,256,3072]{3,2,1,0:T(8,128)(2,1)} %get-tuple-element.38.x0.x1, bf16[2,16,256,3072]{3,2,1,0:T(8,128)(2,1)} %get-tuple-element.38.x0.x1, bf16[384,4096]{1,0:T(8,128)(2,1)} %get-tuple-element.39.refs_0_, ...), custom_call_target="tpu_custom_call" | custom-call | flops 38654705664 | bytes 75000000 | tf_op jit(solution)/shard_map/weight_grad/pallas_call | solution.py:517
  292.1 0.0 collective-permute-start.4
  292.1 0.8 collective-permute-start.5
  293.0 1.2 collective-permute-start.6
  294.2 0.8 collective-permute-start.7
  295.0 1.2 collective-permute-start.1
  296.2 67.3 %collective-permute-done.5.refs_1_ = bf16[384,4096]{1,0:T(8,128)(2,1)} collective-permute-done((bf16[384,4096]{1,0:T(8,128)(2,1)}, bf16[384,4096]{1,0:T(8,128)(2,1)}, u32[]{:S(2)}, u32[]{:S(2)}) %collective-permute-start.5) | collective-permute-done | bytes 3145760 | tf_op jit(solution)/shard_map/ppermute | solution.py:608
  363.5 0.8 collective-permute-start.2
  364.2 1.2 collective-permute-start.3
  365.5 53.8 %weight_grad.5 = (f32[9216,3072]{1,0:T(8,128)}, f32[1536,3072]{1,0:T(8,128)}, bf16[512,1536]{1,0:T(8,128)(2,1)}) custom-call(s32[7]{0:T(128)} %stack.31.tbl.refs_0_, bf16[2,16,256,3072]{3,2,1,0:T(8,128)(2,1)} %get-tuple-element.38.x0.x1, bf16[2,16,256,3072]{3,2,1,0:T(8,128)(2,1)} %get-tuple-element.38.x0.x1, bf16[384,4096]{1,0:T(8,128)(2,1)} %get-tuple-element.48.refs_0_, ...), custom_call_target="tpu_custom_call" | custom-call | flops 38654705664 | bytes 75000000 | tf_op jit(solution)/shard_map/weight_grad/pallas_call | solution.py:517
  419.3 11.1 %collective-permute-done.1.refs_1_ = bf16[384,4096]{1,0:T(8,128)(2,1)} collective-permute-done((bf16[384,4096]{1,0:T(8,128)(2,1)}, bf16[384,4096]{1,0:T(8,128)(2,1)}, u32[]{:S(2)}, u32[]{:S(2)}) %collective-permute-start.1) | collective-permute-done | bytes 3145760 | tf_op jit(solution)/shard_map/ppermute | solution.py:608
  430.4 2.5 collective-permute-done.2.refs_2_
  432.9 0.5 collective-permute-done.3.refs_3_
  433.4 58.1 %weight_grad.6 = (f32[9216,3072]{1,0:T(8,128)}, f32[1536,3072]{1,0:T(8,128)}, bf16[512,1536]{1,0:T(8,128)(2,1)}, f32[3072,3072]{1,0:T(8,128)}) custom-call(s32[7]{0:T(128)} %stack.31.tbl.refs_0_, bf16[2,16,256,3072]{3,2,1,0:T(8,128)(2,1)} %get-tuple-element.38.x0.x1, ...), custom_call_target="tpu_custom_call", output_to_operand_aliasing={{0}: (8, {}), {3}: (9, {})} | custom-call | flops 38654705664 | bytes 75000000 | tf_op jit(solution)/shard_map/weight_grad/pallas_call | solution.py:517
  491.6 1.3 collective-permute-start.8
  492.9 0.8 collective-permute-start.9
  493.6 1.2 collective-permute-start.10
  494.9 67.5 %collective-permute-done.8.refs_1_.refs_5_.refs_9_.refs_13_ = bf16[384,4096]{1,0:T(8,128)(2,1)} collective-permute-done((bf16[384,4096]{1,0:T(8,128)(2,1)}, bf16[384,4096]{1,0:T(8,128)(2,1)}, u32[]{:S(2)}, u32[]{:S(2)}) %collective-permute-start.8) | collective-permute-done | bytes 3145760 | tf_op jit(solution)/shard_map/ppermute | solution.py:608
  562.4 1.0 collective-permute-done.9.refs_2_.refs_6_.refs_10_.refs_14_
  563.4 0.5 collective-permute-done.10.refs_3_.refs_7_.refs_11_.refs_15_
  563.9 63.9 %weight_grad.7 = (f32[9216,3072]{1,0:T(8,128)}, f32[1536,2048]{1,0:T(8,128)}, f32[1536,1024]{1,0:T(8,128)}) custom-call(s32[7]{0:T(128)} %stack.31.tbl.refs_0_, bf16[2,16,256,3072]{3,2,1,0:T(8,128)(2,1)} %get-tuple-element.38.x0.x1, bf16[2,16,256,3072]{3,2,1,0:T(8,128)(2,1)} %get-tuple-element.38.x0.x1, ...), custom_call_target="tpu_custom_call", output_to_operand_aliasing={{0}: (9, {})} | custom-call | flops 38654705664 | bytes 75000000 | tf_op jit(solution)/shard_map/weight_grad/pallas_call | solution.py:517
  627.8 0.5 collective-permute-start.19
  628.3 11.2 %contract.4 = (f32[256,3072]{1,0:T(8,128)}, f32[256,3072]{1,0:T(8,128)}) custom-call(s32[7]{0:T(128)} %stack.31.tbl.refs_0_, bf16[512,1536]{1,0:T(8,128)(2,1)} %get-tuple-element.53.refs_1_, bf16[9216,3072]{1,0:T(8,128)(2,1)} %bitcast.27), custom_call_target="tpu_custom_call" | custom-call | flops 4831838208 | bytes 22000000 | tf_op jit(solution)/shard_map/contract/pallas_call | solution.py:554
  639.4 3.8 collect.1.refs_2_
  643.2 17.7 %contract.5 = (f32[256,3072]{1,0:T(8,128)}, f32[256,3072]{1,0:T(8,128)}) custom-call(s32[7]{0:T(128)} %stack.31.tbl.refs_0_, bf16[512,1536]{1,0:T(8,128)(2,1)} %get-tuple-element.51.refs_1_, bf16[512,1536]{1,0:T(8,128)(2,1)} %collect.1.refs_2_, bf16[9216,3072]{1,0:T(8,128)(2,1)} %bitcast.28, bf16[9216,3072]{1,0:T(8,128)(2,1)} %bitcast.29, ...), custom_call_target="tpu_custom_call" | custom-call | flops 9663676416 | bytes 22000000 | tf_op jit(solution)/shard_map/contract/pallas_call | solution.py:554
  660.9 0.1 collective-permute-start.11
  661.0 11.2 %contract.3 = (f32[256,3072]{1,0:T(8,128)}, f32[256,3072]{1,0:T(8,128)}) custom-call(s32[7]{0:T(128)} %stack.31.tbl.refs_0_, bf16[512,1536]{1,0:T(8,128)(2,1)} %get-tuple-element.43.refs_1_, bf16[3072,3072]{1,0:T(8,128)(2,1)} %bitcast.32), custom_call_target="tpu_custom_call" | custom-call | flops 4831838208 | bytes 22000000 | tf_op jit(solution)/shard_map/contract/pallas_call | solution.py:554
  672.2 0.5 collective-permute-start
  672.6 1.5 select_reduce_fusion
  674.1 0.6 broadcast_in_dim.7
  674.8 1.3 dynamic_update_slice.9
  676.1 8.0 %finish.3 = (bf16[2,128,3072]{2,1,0:T(8,128)(2,1)}, f32[8,3072]{1,0:T(8,128)}) custom-call(f32[256,3072]{1,0:T(8,128)} %get-tuple-element.56.du_own, f32[256,3072]{1,0:T(8,128)} %collective-permute-done.11.du_peer, bf16[2,128,3072]{2,1,0:T(8,128)(2,1)} %x_ref.3, bf16[2,128,3072]{2,1,0:T(8,128)(2,1)} %gy_ref.1, f32[8,3072]{1,0:T(8,128)} %bitcast.16.db_ref, ...), custom_call_target="tpu_custom_call" | custom-call | flops 100000000 | bytes 10000000 | tf_op jit(solution)/shard_map/finish/pallas_call | solution.py:593
  684.0 1.2 collective-permute-start.12
  685.3 3.7 collective-permute-done.12
  689.0 0.9 add.42
  689.9 1.3 collective-permute-start.13
  691.2 3.4 collective-permute-done.13
  694.6 1.3 collective-permute-start.14
  695.9 3.4 collective-permute-done.14
  699.2 0.6 add.44
  699.9 4.4 finish.2
  704.3 1.0 add.45
  705.2 0.7 reshape.80
  706.0 0.6 fusion
  706.6 11.5 %constant_dynamic-update-slice_fusion.1 = f32[9216,3072]{1,0:T(8,128)} fusion(f32[9216,3072]{1,0:T(8,128)} %get-tuple-element.64, f32[1536,2048]{1,0:T(8,128)} %collective-permute-done.18, s32[]{:T(128)S(6)} %select_n.58), kind=kLoop, calls=%fused_computation.2 | loop fusion | bytes 25165828 | tf_op jit(solution)/shard_map/dynamic_update_slice | solution.py:657
  718.1 6.6 constant_dynamic-update-slice_fusion
  (16 shorter events, 0.2 us)
Async XLA Ops:
  292.1 141.3 %collective-permute-start.4 = (f32[1536,3072]{1,0:T(8,128)}, f32[1536,3072]{1,0:T(8,128)}, u32[]{:S(2)}, u32[]{:S(2)}) collective-permute-start(f32[1536,3072]{1,0:T(8,128)} %get-tuple-element.47), channel_id=1, source_target_pairs={{0,1},{1,0},{2,3},{3,2},{4,5},{5,4},{6,7},{7,6},{8,9},{9,8},{10,11... | collective-permute-start | bytes 56623112 | tf_op jit(solution)/shard_map/ppermute | solution.py:608
  292.1 71.3 %collective-permute-start.5 = (bf16[384,4096]{1,0:T(8,128)(2,1)}, bf16[384,4096]{1,0:T(8,128)(2,1)}, u32[]{:S(2)}, u32[]{:S(2)}) collective-permute-start(bf16[384,4096]{1,0:T(8,128)(2,1)} %get-tuple-element.48.refs_0_), channel_id=1, source_target_pairs={{0,2},{1,3},{2,0},{3,1},{4,6},{5,7},{6,4},{7,5},{8,10},{9,11},{10,... | collective-permute-start | bytes 9437192 | tf_op jit(solution)/shard_map/ppermute | solution.py:608
  293.0 71.3 %collective-permute-start.6 = (bf16[384,4096]{1,0:T(8,128)(2,1)}, bf16[384,4096]{1,0:T(8,128)(2,1)}, u32[]{:S(2)}, u32[]{:S(2)}) collective-permute-start(bf16[384,4096]{1,0:T(8,128)(2,1)} %get-tuple-element.48.refs_0_), channel_id=1, source_target_pairs={{0,4},{1,5},{2,6},{3,7},{4,0},{5,1},{6,2},{7,3},{8,12},{9,13},{10,... | collective-permute-start | bytes 9437192 | tf_op jit(solution)/shard_map/ppermute | solution.py:608
  294.2 71.3 %collective-permute-start.7 = (bf16[384,4096]{1,0:T(8,128)(2,1)}, bf16[384,4096]{1,0:T(8,128)(2,1)}, u32[]{:S(2)}, u32[]{:S(2)}) collective-permute-start(bf16[384,4096]{1,0:T(8,128)(2,1)} %get-tuple-element.48.refs_0_), channel_id=1, source_target_pairs={{0,8},{1,9},{2,10},{3,11},{4,12},{5,13},{6,14},{7,15},{8,0},{9,1},... | collective-permute-start | bytes 9437192 | tf_op jit(solution)/shard_map/ppermute | solution.py:608
  295.0 135.4 %collective-permute-start.1 = (bf16[384,4096]{1,0:T(8,128)(2,1)}, bf16[384,4096]{1,0:T(8,128)(2,1)}, u32[]{:S(2)}, u32[]{:S(2)}) collective-permute-start(bf16[384,4096]{1,0:T(8,128)(2,1)} %get-tuple-element.46.refs_0_), channel_id=1, source_target_pairs={{0,2},{1,3},{2,0},{3,1},{4,6},{5,7},{6,4},{7,5},{8,10},{9,11},{10,... | collective-permute-start | bytes 9437192 | tf_op jit(solution)/shard_map/ppermute | solution.py:608
  363.5 69.4 %collective-permute-start.2 = (bf16[384,4096]{1,0:T(8,128)(2,1)}, bf16[384,4096]{1,0:T(8,128)(2,1)}, u32[]{:S(2)}, u32[]{:S(2)}) collective-permute-start(bf16[384,4096]{1,0:T(8,128)(2,1)} %get-tuple-element.46.refs_0_), channel_id=1, source_target_pairs={{0,4},{1,5},{2,6},{3,7},{4,0},{5,1},{6,2},{7,3},{8,12},{9,13},{10,... | collective-permute-start | bytes 9437192 | tf_op jit(solution)/shard_map/ppermute | solution.py:608
  364.2 69.1 %collective-permute-start.3 = (bf16[384,4096]{1,0:T(8,128)(2,1)}, bf16[384,4096]{1,0:T(8,128)(2,1)}, u32[]{:S(2)}, u32[]{:S(2)}) collective-permute-start(bf16[384,4096]{1,0:T(8,128)(2,1)} %get-tuple-element.46.refs_0_), channel_id=1, source_target_pairs={{0,8},{1,9},{2,10},{3,11},{4,12},{5,13},{6,14},{7,15},{8,0},{9,1},... | collective-permute-start | bytes 9437192 | tf_op jit(solution)/shard_map/ppermute | solution.py:608
  419.2 144.6 %collective-permute-start.16 = (f32[1536,3072]{1,0:T(8,128)}, f32[1536,3072]{1,0:T(8,128)}, u32[]{:S(2)}, u32[]{:S(2)}) collective-permute-start(f32[1536,3072]{1,0:T(8,128)} %get-tuple-element.61), channel_id=1, source_target_pairs={{0,1},{1,0},{2,3},{3,2},{4,5},{5,4},{6,7},{7,6},{8,9},{9,8},{10,11... | collective-permute-start | bytes 56623112 | tf_op jit(solution)/shard_map/ppermute | solution.py:608
  491.5 72.4 %collective-permute-start.17 = (f32[1536,3072]{1,0:T(8,128)}, f32[1536,3072]{1,0:T(8,128)}, u32[]{:S(2)}, u32[]{:S(2)}) collective-permute-start(f32[1536,3072]{1,0:T(8,128)} %get-tuple-element.62), channel_id=1, source_target_pairs={{0,1},{1,0},{2,3},{3,2},{4,5},{5,4},{6,7},{7,6},{8,9},{9,8},{10,11... | collective-permute-start | bytes 56623112 | tf_op jit(solution)/shard_map/ppermute | solution.py:608
  491.6 70.8 %collective-permute-start.8 = (bf16[384,4096]{1,0:T(8,128)(2,1)}, bf16[384,4096]{1,0:T(8,128)(2,1)}, u32[]{:S(2)}, u32[]{:S(2)}) collective-permute-start(bf16[384,4096]{1,0:T(8,128)(2,1)} %get-tuple-element.52.refs_0_.refs_4_.refs_8_.refs_12_), channel_id=1, source_target_pairs={{0,2},{1,3},{2,0},{3,1},{4,6},{5,7},{6,4},{7,5},{8,10},{9,11},{10,... | collective-permute-start | bytes 9437192 | tf_op jit(solution)/shard_map/ppermute | solution.py:608
  492.9 70.5 %collective-permute-start.9 = (bf16[384,4096]{1,0:T(8,128)(2,1)}, bf16[384,4096]{1,0:T(8,128)(2,1)}, u32[]{:S(2)}, u32[]{:S(2)}) collective-permute-start(bf16[384,4096]{1,0:T(8,128)(2,1)} %get-tuple-element.52.refs_0_.refs_4_.refs_8_.refs_12_), channel_id=1, source_target_pairs={{0,4},{1,5},{2,6},{3,7},{4,0},{5,1},{6,2},{7,3},{8,12},{9,13},{10,... | collective-permute-start | bytes 9437192 | tf_op jit(solution)/shard_map/ppermute | solution.py:608
  493.6 70.2 %collective-permute-start.10 = (bf16[384,4096]{1,0:T(8,128)(2,1)}, bf16[384,4096]{1,0:T(8,128)(2,1)}, u32[]{:S(2)}, u32[]{:S(2)}) collective-permute-start(bf16[384,4096]{1,0:T(8,128)(2,1)} %get-tuple-element.52.refs_0_.refs_4_.refs_8_.refs_12_), channel_id=1, source_target_pairs={{0,8},{1,9},{2,10},{3,11},{4,12},{5,13},{6,14},{7,15},{8,0},{9,1},... | collective-permute-start | bytes 9437192 | tf_op jit(solution)/shard_map/ppermute | solution.py:608
  627.7 78.9 %collective-permute-start.18 = (f32[1536,2048]{1,0:T(8,128)}, f32[1536,2048]{1,0:T(8,128)}, u32[]{:S(2)}, u32[]{:S(2)}) collective-permute-start(f32[1536,2048]{1,0:T(8,128)} %get-tuple-element.65), channel_id=1, source_target_pairs={{0,1},{1,0},{2,3},{3,2},{4,5},{5,4},{6,7},{7,6},{8,9},{9,8},{10,11... | collective-permute-start | bytes 37748744 | tf_op jit(solution)/shard_map/ppermute | solution.py:608
  627.8 90.4 %collective-permute-start.19 = (f32[1536,1024]{1,0:T(8,128)}, f32[1536,1024]{1,0:T(8,128)}, u32[]{:S(2)}, u32[]{:S(2)}) collective-permute-start(f32[1536,1024]{1,0:T(8,128)} %get-tuple-element.66), channel_id=1, source_target_pairs={{0,1},{1,0},{2,3},{3,2},{4,5},{5,4},{6,7},{7,6},{8,9},{9,8},{10,11... | collective-permute-start | bytes 18874376 | tf_op jit(solution)/shard_map/ppermute | solution.py:608
  660.9 15.1 %collective-permute-start.11 = (f32[256,3072]{1,0:T(8,128)}, f32[256,3072]{1,0:T(8,128)}, u32[]{:S(2)}, u32[]{:S(2)}) collective-permute-start(f32[256,3072]{1,0:T(8,128)} %get-tuple-element.57), channel_id=1, source_target_pairs={{0,1},{1,0},{2,3},{3,2},{4,5},{5,4},{6,7},{7,6},{8,9},{9,8},{10,11... | collective-permute-start | bytes 9437192 | tf_op jit(solution)/shard_map/ppermute | solution.py:608
  672.2 27.7 %collective-permute-start = (f32[256,3072]{1,0:T(8,128)}, f32[256,3072]{1,0:T(8,128)}, u32[]{:S(2)}, u32[]{:S(2)}) collective-permute-start(f32[256,3072]{1,0:T(8,128)} %get-tuple-element.45), channel_id=1, source_target_pairs={{0,1},{1,0},{2,3},{3,2},{4,5},{5,4},{6,7},{7,6},{8,9},{9,8},{10,11... | collective-permute-start | bytes 9437192 | tf_op jit(solution)/shard_map/ppermute | solution.py:608
  684.0 5.0 collective-permute-start.12
  689.9 4.7 collective-permute-start.13
  694.6 4.7 collective-permute-start.14
  699.9 4.4 collective-permute-start.15
